TPU v7x, 128 devices: a whole 4x4x4 slice. The times are simulated.
128 devices in a mesh: dom: 128 (over y, x, z, core).
Axes of the slice: x: 4, y: 4, z: 4, core: 2. Of those that a mesh axis runs over, the one named last changes fastest.
Arguments:
- start_point: float32 [65536, 128], P('dom'), may hold values from -6 to 6
- residual: float32 [65536, 128], P('dom'), may hold values from -40 to 40
- direction: float32 [65536, 128], P('dom'), may hold values from -40 to 40
- send_list: int32 [128, 4, 3], P('dom'), may hold values from 0 to 3, as said below
- block_cols: int32 [512, 6], P('dom'), may hold values from 0 to 15, as said below
- block_vals: float32 [512, 6, 128, 128], P('dom'), may hold values from -0.2 to 8.1, as said below
Outputs:
- new_point: float32 [65536, 128], P('dom')
- new_residual: float32 [65536, 128], P('dom')
- new_direction: float32 [65536, 128], P('dom')
Inputs may be any that keep to these rules, and one draw needn't show every extreme that they name: send_list[t, m] lists, in its first entries, the distinct blocks of partition t that the partition at offset -off (off as in the first step) reads; between 1 and 3 of them are read for each pair, and some pair reads 3; the other entries are valid block numbers that are never read. `block_cols`: entry 0 of a block row names the row's own block; a block that couples two partitions appears in both partitions' rows, transposed; the assembled matrix is symmetric positive definite. `block_vals`: stored blocks that no coupling uses are zero.
All inputs are finite; a program needn't handle non-finite values.
Results may differ from a plain program's by a relative error of at most 0.0003.
Values sent between devices are 32-bit elements; how exact they have to be, the bound alone decides.
A program may use at most 128 MiB of HBM per device.

v0:
```python
import jax
import jax.numpy as jnp
from jax import lax
from jax.sharding import Mesh
from jax.sharding import PartitionSpec as P

STEPS = 6
BASIS = 13
DOM = ("dom_0", "dom_1", "dom_2", "dom_3")


center_value = 4.5
half_range = 4.5


def from_behind(shard, axis, by):
    peers = lax.axis_size(axis)
    return lax.ppermute(shard, axis, [(i, (i + by) % peers) for i in range(peers)])


def in_blocks(shard, dim, peers):
    lengths = shard.shape
    pieces = shard.reshape(*lengths[:dim], peers, lengths[dim] // peers, *lengths[dim + 1 :])
    return jnp.moveaxis(pieces, dim, 0)


def sum_at_owner(shard, axis, dim):
    peers = lax.axis_size(axis)
    pieces = lax.all_to_all(in_blocks(shard, dim, peers), axis, 0, 0, tiled=True)
    return jnp.sum(pieces, axis=0)


def sum_by_axis(shard, axes, dim):
    far, near = axes
    own = sum_at_owner(in_blocks(shard, dim, lax.axis_size(far)), near, dim + 1)
    return jnp.sum(lax.all_to_all(own, far, 0, 0, tiled=True), axis=0)


def filled_up(lines, peers):
    spare = -len(lines) % peers
    return jnp.pad(lines, [(0, spare)] + [(0, 0)] * (lines.ndim - 1))


def sent_to_all(shard, axis):
    peers = lax.axis_size(axis)
    return lax.all_to_all(
        jnp.broadcast_to(shard[None], (peers, *shard.shape)), axis, 0, 0, tiled=True
    )


def joined_along(pieces, dim):
    lengths = list(pieces.shape[1:])
    lengths[dim] *= pieces.shape[0]
    return jnp.moveaxis(pieces, 0, dim).reshape(lengths)


def whole_of(shard, axes, dim):
    far, near = axes
    pieces = sent_to_all(sent_to_all(shard, far), near)
    return joined_along(pieces.swapaxes(0, 1).reshape(-1, *shard.shape), dim)


def sum_by_parts(shard, axes):
    lines = shard.reshape(-1, shard.shape[-1])
    own = sum_by_axis(filled_up(lines, lax.axis_size(axes[0]) * lax.axis_size(axes[1])), axes, 0)
    whole = whole_of(own, axes, 0)
    return whole[: len(lines)].reshape(shard.shape)


def apply_blocks(blocked, send_rows, block_cols, block_vals):
    block_count, block_rows, width = blocked.shape
    highest = lax.Precision.HIGHEST
    flat_rows = blocked.reshape(block_count, block_rows * width)
    hop_count = send_rows.shape[0] // 2
    own_ids = jnp.arange(block_count, dtype=jnp.int32)
    pieces = [flat_rows]
    for slot_index in range(2 * hop_count):
        offset = slot_index + 1 if slot_index < hop_count else hop_count - 1 - slot_index
        chooser = (send_rows[slot_index][:, None] == own_ids[None, :]).astype(jnp.float32)
        outgoing = jnp.dot(chooser, flat_rows, precision=highest)
        pieces.append(from_behind(outgoing, DOM, -offset))
    ghost_table = jnp.concatenate(pieces, axis=0)
    ghost_ids = jnp.arange(ghost_table.shape[0], dtype=jnp.int32)
    running = jnp.zeros((block_count, block_rows, width), jnp.float32)
    for slot_index in range(block_cols.shape[1]):
        chooser = (block_cols[:, slot_index][:, None] == ghost_ids[None, :]).astype(jnp.float32)
        picked = jnp.dot(chooser, ghost_table, precision=highest).reshape(
            block_count, block_rows, width
        )
        running = running + jnp.einsum(
            "icb,ibw->icw", block_vals[:, slot_index], picked, precision=highest
        )
    return running


def next_vector(vector, send_rows, block_cols, block_vals):
    block_count = block_vals.shape[0]
    block_rows = block_vals.shape[2]
    blocked = vector.reshape(block_count, block_rows, vector.shape[1])
    image_part = apply_blocks(blocked, send_rows, block_cols, block_vals).reshape(vector.shape)
    return (image_part - center_value * vector) / half_range


def basis_change():
    positions = jnp.arange(BASIS)
    row_ids = positions[:, None]
    col_ids = positions[None, :]
    active = (col_ids < STEPS) | (col_ids > STEPS) & (col_ids < BASIS - 1)
    change_table = jnp.where(active & (row_ids == col_ids), center_value, 0.0)
    change_table = change_table + jnp.where(active & (row_ids == col_ids + 1), half_range, 0.0)
    return change_table.astype(jnp.float32)


def coefficient_steps(gram_matrix):
    change_table = basis_change()
    column_count = gram_matrix.shape[0]
    positions = jnp.arange(BASIS)
    point_c = jnp.zeros((column_count, BASIS), jnp.float32)
    resid_c = jnp.broadcast_to((positions == STEPS + 1).astype(jnp.float32), (column_count, BASIS))
    direc_c = jnp.broadcast_to((positions == 0).astype(jnp.float32), (column_count, BASIS))
    highest = lax.Precision.HIGHEST
    for step_index in range(STEPS):
        current = jnp.sum(
            resid_c * jnp.einsum("nab,nb->na", gram_matrix, resid_c, precision=highest), axis=1
        )
        moved_dir = jnp.einsum("ab,nb->na", change_table, direc_c, precision=highest)
        curvature = jnp.sum(
            direc_c * jnp.einsum("nab,nb->na", gram_matrix, moved_dir, precision=highest), axis=1
        )
        alpha_step = current / curvature
        point_c = point_c + alpha_step[:, None] * direc_c
        resid_c = resid_c - alpha_step[:, None] * moved_dir
        following = jnp.sum(
            resid_c * jnp.einsum("nab,nb->na", gram_matrix, resid_c, precision=highest), axis=1
        )
        direc_c = resid_c + (following / current)[:, None] * direc_c
    return (point_c, resid_c, direc_c)


def shards(start_point, residual, direction, send_list, block_cols, block_vals):
    send_rows = send_list[0]
    rhs_width = residual.shape[1]
    p_basis = [direction]
    r_basis = [residual]
    both_sets = jnp.concatenate([direction, residual], axis=1)
    for power_step in range(STEPS - 1):
        both_sets = next_vector(both_sets, send_rows, block_cols, block_vals)
        p_basis.append(both_sets[:, :rhs_width])
        r_basis.append(both_sets[:, rhs_width:])
    p_basis.append(next_vector(p_basis[-1], send_rows, block_cols, block_vals))
    basis_stack = jnp.stack(p_basis + r_basis)
    local_gram = jnp.einsum(
        "arn,brn->nab", basis_stack, basis_stack, precision=lax.Precision.HIGHEST
    )
    gram_matrix = sum_by_parts(local_gram, (("dom_0", "dom_1", "dom_2"), "dom_3"))
    point_c, resid_c, direc_c = coefficient_steps(gram_matrix)
    highest = lax.Precision.HIGHEST
    new_point = start_point + jnp.einsum("na,arn->rn", point_c, basis_stack, precision=highest)
    new_residual = jnp.einsum("na,arn->rn", resid_c, basis_stack, precision=highest)
    new_direction = jnp.einsum("na,arn->rn", direc_c, basis_stack, precision=highest)
    return (new_point, new_residual, new_direction)


def solution(mesh):
    finer = Mesh(mesh.devices.reshape(4, 4, 4, 2), ("dom_0", "dom_1", "dom_2", "dom_3"))
    placed = (
        P(DOM, None),
        P(DOM, None),
        P(DOM, None),
        P(DOM, None, None),
        P(DOM, None),
        P(DOM, None, None, None),
    )
    return jax.shard_map(
        shards,
        mesh=finer,
        in_specs=placed,
        out_specs=(P(DOM, None), P(DOM, None), P(DOM, None)),
        check_vma=False,
    )
```

profile of v0, /device:TPU:1, one launch (start us, length us, event | category | flops | bytes accessed | tf_op | source)
XLA Modules:
  0.0 382.5 jit_solution(6092274086660090943)
XLA Ops:
  0.6 1.1 copy.126
  1.7 1.1 copy.127
  4.4 1.4 collective-permute-start
  6.5 8.6 %collective-permute-start.1 = (f32[3,32768]{1,0:T(4,128)S(1)}, f32[3,32768]{1,0:T(4,128)}, u32[]{:S(2)}, u32[]{:S(2)}) collective-permute-start(f32[3,32768]{1,0:T(4,128)S(1)} %fusion.240), channel_id=1, source_target_pairs={{0,126},{1,127},{2,0},{3,1},{4,2},{5,3},{6,4},{7,5},{8,6},{9,7},{1... | collective-permute-start | bytes 1179656 | tf_op jit(solution)/shard_map/ppermute | solution.py:18
  15.7 1.4 collective-permute-start.2
  18.1 1.3 collective-permute-done
  19.4 7.4 %collective-permute-done.1 = f32[3,32768]{1,0:T(4,128)} collective-permute-done((f32[3,32768]{1,0:T(4,128)S(1)}, f32[3,32768]{1,0:T(4,128)}, u32[]{:S(2)}, u32[]{:S(2)}) %collective-permute-start.1) | collective-permute-done | bytes 393248 | tf_op jit(solution)/shard_map/ppermute | solution.py:18
  28.4 12.4 %collective-permute-done.3 = f32[3,32768]{1,0:T(4,128)} collective-permute-done((f32[3,32768]{1,0:T(4,128)S(1)}, f32[3,32768]{1,0:T(4,128)}, u32[]{:S(2)}, u32[]{:S(2)}) %collective-permute-start.3) | collective-permute-done | bytes 393248 | tf_op jit(solution)/shard_map/ppermute | solution.py:18
  40.8 10.6 %concatenate.22 = f32[16,32768]{1,0:T(8,128)S(1)} concatenate(f32[4,32768]{1,0:T(4,128)S(1)} %reshape_reshape.6, f32[3,32768]{1,0:T(4,128)S(1)} %collective-permute-done, f32[3,32768]{1,0:T(4,128)} %collective-permute-done.1, f32[3,32768]{1,0:T(4,128)} %copy-done.32, f32[3,32768]{1,0:T(4,128)} %collective-permute-done.3), dimensions={0} | concatenate | bytes 4194304 | tf_op jit(solution)/shard_map/concatenate | solution.py:82
  63.0 1.1 fusion.245
  64.3 1.4 collective-permute-start.7
  66.4 11.7 %collective-permute-done.5 = f32[3,32768]{1,0:T(4,128)S(1)} collective-permute-done((f32[3,32768]{1,0:T(4,128)S(1)}, f32[3,32768]{1,0:T(4,128)S(1)}, u32[]{:S(2)}, u32[]{:S(2)}) %collective-permute-start.5) | collective-permute-done | bytes 393248 | tf_op jit(solution)/shard_map/ppermute | solution.py:18
  78.1 10.7 %collective-permute-done.7 = f32[3,32768]{1,0:T(4,128)S(1)} collective-permute-done((f32[3,32768]{1,0:T(4,128)S(1)}, f32[3,32768]{1,0:T(4,128)S(1)}, u32[]{:S(2)}, u32[]{:S(2)}) %collective-permute-start.7) | collective-permute-done | bytes 393248 | tf_op jit(solution)/shard_map/ppermute | solution.py:18
  89.7 12.1 %concatenate.23 = f32[16,32768]{1,0:T(8,128)S(1)} concatenate(f32[4,32768]{1,0:T(4,128)S(1)} %broadcast_multiply_fusion.2, f32[3,32768]{1,0:T(4,128)} %collective-permute-done.4, f32[3,32768]{1,0:T(4,128)} %copy-done.34, f32[3,32768]{1,0:T(4,128)} %copy-done.37, f32[3,32768]{1,0:T(4,128)} %copy-done.40), dimensions={0} | concatenate | bytes 4194304 | tf_op jit(solution)/shard_map/concatenate | solution.py:82
  114.9 6.9 %collective-permute-start.9 = (f32[3,32768]{1,0:T(4,128)S(1)}, f32[3,32768]{1,0:T(4,128)S(1)}, u32[]{:S(2)}, u32[]{:S(2)}) collective-permute-start(f32[3,32768]{1,0:T(4,128)S(1)} %fusion.238), channel_id=1, source_target_pairs={{0,126},{1,127},{2,0},{3,1},{4,2},{5,3},{6,4},{7,5},{8,6},{9,7},{1... | collective-permute-start | bytes 1179656 | tf_op jit(solution)/shard_map/ppermute | solution.py:18
  122.8 3.1 collective-permute-done.10
  125.9 9.7 %collective-permute-done.11 = f32[3,32768]{1,0:T(4,128)S(1)} collective-permute-done((f32[3,32768]{1,0:T(4,128)S(1)}, f32[3,32768]{1,0:T(4,128)S(1)}, u32[]{:S(2)}, u32[]{:S(2)}) %collective-permute-start.11) | collective-permute-done | bytes 393248 | tf_op jit(solution)/shard_map/ppermute | solution.py:18
  137.2 12.1 %concatenate.24 = f32[16,32768]{1,0:T(8,128)S(1)} concatenate(f32[4,32768]{1,0:T(4,128)S(1)} %broadcast_multiply_fusion.1, f32[3,32768]{1,0:T(4,128)} %collective-permute-done.8, f32[3,32768]{1,0:T(4,128)} %copy-done.41, f32[3,32768]{1,0:T(4,128)} %copy-done.35, f32[3,32768]{1,0:T(4,128)} %copy-done.38), dimensions={0} | concatenate | bytes 4194304 | tf_op jit(solution)/shard_map/concatenate | solution.py:82
  159.2 1.2 broadcast_multiply_fusion
  161.7 1.1 fusion.225
  163.5 9.5 %collective-permute-start.13 = (f32[3,32768]{1,0:T(4,128)S(1)}, f32[3,32768]{1,0:T(4,128)S(1)}, u32[]{:S(2)}, u32[]{:S(2)}) collective-permute-start(f32[3,32768]{1,0:T(4,128)S(1)} %fusion.237), channel_id=1, source_target_pairs={{0,126},{1,127},{2,0},{3,1},{4,2},{5,3},{6,4},{7,5},{8,6},{9,7},{1... | collective-permute-start | bytes 1179656 | tf_op jit(solution)/shard_map/ppermute | solution.py:18
  173.5 7.5 %collective-permute-done.13 = f32[3,32768]{1,0:T(4,128)S(1)} collective-permute-done((f32[3,32768]{1,0:T(4,128)S(1)}, f32[3,32768]{1,0:T(4,128)S(1)}, u32[]{:S(2)}, u32[]{:S(2)}) %collective-permute-start.13) | collective-permute-done | bytes 393248 | tf_op jit(solution)/shard_map/ppermute | solution.py:18
  181.0 3.1 collective-permute-done.14
  184.0 9.6 %collective-permute-done.15 = f32[3,32768]{1,0:T(4,128)S(1)} collective-permute-done((f32[3,32768]{1,0:T(4,128)S(1)}, f32[3,32768]{1,0:T(4,128)S(1)}, u32[]{:S(2)}, u32[]{:S(2)}) %collective-permute-start.15) | collective-permute-done | bytes 393248 | tf_op jit(solution)/shard_map/ppermute | solution.py:18
  195.2 12.1 %concatenate.25 = f32[16,32768]{1,0:T(8,128)S(1)} concatenate(f32[4,32768]{1,0:T(4,128)S(1)} %copy-done.24, f32[3,32768]{1,0:T(4,128)} %copy-done.42, f32[3,32768]{1,0:T(4,128)} %copy-done.33, f32[3,32768]{1,0:T(4,128)} %copy-done.36, f32[3,32768]{1,0:T(4,128)} %copy-done.39), dimensions={0} | concatenate | bytes 4194304 | tf_op jit(solution)/shard_map/concatenate | solution.py:82
  217.1 1.4 fusion.236
  218.5 1.4 fusion.230
  220.0 1.5 fusion.224
  221.4 1.6 fusion.242
  223.1 1.7 collective-permute-start.18
  229.0 1.0 copy.137
  230.3 6.5 %collective-permute-done.17 = f32[3,32768]{1,0:T(4,128)} collective-permute-done((f32[3,32768]{1,0:T(4,128)}, f32[3,32768]{1,0:T(4,128)}, u32[]{:S(2)}, u32[]{:S(2)}) %collective-permute-start.17) | collective-permute-done | bytes 393248 | tf_op jit(solution)/shard_map/ppermute | solution.py:18
  236.8 11.3 %collective-permute-done.19 = f32[3,32768]{1,0:T(4,128)} collective-permute-done((f32[3,32768]{1,0:T(4,128)}, f32[3,32768]{1,0:T(4,128)}, u32[]{:S(2)}, u32[]{:S(2)}) %collective-permute-start.19) | collective-permute-done | bytes 393248 | tf_op jit(solution)/shard_map/ppermute | solution.py:18
  248.1 12.1 %concatenate.26 = f32[16,32768]{1,0:T(8,128)S(1)} concatenate(f32[4,32768]{1,0:T(4,128)S(1)} %subtract_multiply_fusion.1, f32[3,32768]{1,0:T(4,128)} %collective-permute-done.16, f32[3,32768]{1,0:T(4,128)} %collective-permute-done.17, f32[3,32768]{1,0:T(4,128)} %collective-permute-done.18, f32[3,32768]{1,0:T(4,128)} %collective-permute-done.19), dimensions={0} | concatenate | bytes 4194304 | tf_op jit(solution)/shard_map/concatenate | solution.py:82
  270.4 2.5 subtract_multiply_fusion
  275.0 1.9 collective-permute-start.22
  277.0 1.4 collective-permute-start.23
  284.5 7.1 %collective-permute-done.23 = f32[3,16384]{1,0:T(4,128)} collective-permute-done((f32[3,16384]{1,0:T(4,128)S(1)}, f32[3,16384]{1,0:T(4,128)}, u32[]{:S(2)}, u32[]{:S(2)}) %collective-permute-start.23) | collective-permute-done | bytes 196640 | tf_op jit(solution)/shard_map/ppermute | solution.py:18
  291.6 6.6 %concatenate.27 = f32[16,16384]{1,0:T(8,128)S(1)} concatenate(f32[4,16384]{1,0:T(4,128)S(1)} %reshape_reshape.14, f32[3,16384]{1,0:T(4,128)} %copy-done.44, f32[3,16384]{1,0:T(4,128)} %copy-done.45, f32[3,16384]{1,0:T(4,128)} %copy-done.46, f32[3,16384]{1,0:T(4,128)} %collective-permute-done.23), dimensions={0} | concatenate | bytes 2097152 | tf_op jit(solution)/shard_map/concatenate | solution.py:82
  304.8 8.8 %stack.55 = f32[13,512,128]{1,0,2:T(8,128)} concatenate(f32[1,512,128]{1,0,2:T(1,128)S(1)} %copy-done.28, f32[1,512,128]{1,0,2:T(1,128)S(1)} %copy.143, f32[1,512,128]{1,0,2:T(1,128)S(1)} %copy.144, f32[1,512,128]{1,0,2:T(1,128)S(1)} %copy.145, f32[1,512,128]{1,0,2:T(1,128)S(1)} %copy.146, f32[1,512,128]{1,0,2:T(1,128)S(1)} %copy.147, f32[1,512,128]{1,0,2:T(1,128)S(1)} %copy.148, ...), dimensions={0} | concatenate | bytes 6815744 | tf_op jit(solution)/shard_map/stack | solution.py:151
  313.6 9.0 %fusion.327 = f32[128,13,13]{2,1,0:T(8,128)S(1)} fusion(f32[13,512,128]{1,0,2:T(8,128)} %stack.55), kind=kOutput, calls=%fused_computation.447 | convolution fusion | flops 132907008 | bytes 3494400 | tf_op jit(solution)/shard_map/arn,brn->nab/dot_general | solution.py:152
  323.3 3.6 all_to_all.20
  329.9 4.6 %all-to-all-start.1 = ((f32[64,1,169]{2,1,0:T(1,128)}), f32[64,1,169]{2,1,0:T(1,128)S(1)}, u32[]{:S(2)}, u32[]{:S(2)}) async-start(f32[64,1,169]{2,1,0:T(1,128)} %reshape.342), calls=%async_computation.1 | async-start | bytes 131072 | tf_op jit(solution)/shard_map/all_to_all | solution.py:36
  334.7 8.2 %all-to-all-done.1 = f32[64,1,169]{2,1,0:T(1,128)S(1)} async-done(((f32[64,1,169]{2,1,0:T(1,128)}), f32[64,1,169]{2,1,0:T(1,128)S(1)}, u32[]{:S(2)}, u32[]{:S(2)}) %all-to-all-start.1) | async-done | bytes 43296 | tf_op jit(solution)/shard_map/all_to_all | solution.py:36
  345.1 5.0 %all-to-all-start.2 = ((f32[64,1,169]{2,1,0:T(1,128)}), f32[64,1,169]{2,1,0:T(1,128)S(1)}, u32[]{:S(2)}, u32[]{:S(2)}) async-start(f32[64,1,169]{2,1,0:T(1,128)} %reshape.344), calls=%async_computation.2 | async-start | bytes 131072 | tf_op jit(solution)/shard_map/all_to_all | solution.py:46
  350.2 8.3 %all-to-all-done.2 = f32[64,1,169]{2,1,0:T(1,128)S(1)} async-done(((f32[64,1,169]{2,1,0:T(1,128)}), f32[64,1,169]{2,1,0:T(1,128)S(1)}, u32[]{:S(2)}, u32[]{:S(2)}) %all-to-all-start.2) | async-done | bytes 43296 | tf_op jit(solution)/shard_map/all_to_all | solution.py:46
  360.0 6.1 %all_to_all.21 = f32[2,1,10816]{2,1,0:T(1,128)S(1)} all-to-all(f32[2,1,10816]{2,1,0:T(1,128)S(1)} %reshape.346), channel_id=1, replica_groups=mesh['dom_0'=4,'dom_1'=4,'dom_2'=4,'dom_3'=2] {'dom_3'}, dimensions={0} | all-to-all | bytes 173056 | tf_op jit(solution)/shard_map/all_to_all | solution.py:46
  375.5 4.3 %multiply_reduce_fusion = (f32[128,512]{1,0:T(8,128)S(1)}, f32[128,512]{1,0:T(8,128)S(1)}, f32[128,512]{1,0:T(8,128)S(1)}) fusion(f32[13,512,128]{1,0,2:T(8,128)} %stack.55, f32[128,13]{1,0:T(8,128)S(1)} %copy.282, f32[128,13]{1,0:T(8,128)S(1)} %copy.280, f32[128,13]{1,0:T(8,128)S(1)} %copy.277), kind=kLoop, calls=%fused_computation | loop fusion | flops 4915200 | bytes 4214272
  (349 shorter events, 106.0 us)
Async XLA Ops:
  0.6 2.7 copy-start.48
  3.7 14.1 %copy-start.47 = (s32[4,6]{1,0:T(4,128)S(1)}, s32[4,6]{1,0:T(4,128)}, u32[]{:S(2)}) copy-start(s32[4,6]{1,0:T(4,128)} %param.10) | copy-start | bytes 292
  4.4 15.0 %collective-permute-start = (f32[3,32768]{1,0:T(4,128)S(1)}, f32[3,32768]{1,0:T(4,128)S(1)}, u32[]{:S(2)}, u32[]{:S(2)}) collective-permute-start(f32[3,32768]{1,0:T(4,128)S(1)} %fusion.246), channel_id=1, source_target_pairs={{0,127},{1,0},{2,1},{3,2},{4,3},{5,4},{6,5},{7,6},{8,7},{9,8},{10,... | collective-permute-start | bytes 1179656 | tf_op jit(solution)/shard_map/ppermute | solution.py:18
  6.5 20.3 %collective-permute-start.1 = (f32[3,32768]{1,0:T(4,128)S(1)}, f32[3,32768]{1,0:T(4,128)}, u32[]{:S(2)}, u32[]{:S(2)}) collective-permute-start(f32[3,32768]{1,0:T(4,128)S(1)} %fusion.240), channel_id=1, source_target_pairs={{0,126},{1,127},{2,0},{3,1},{4,2},{5,3},{6,4},{7,5},{8,6},{9,7},{1... | collective-permute-start | bytes 1179656 | tf_op jit(solution)/shard_map/ppermute | solution.py:18
  15.7 11.9 %collective-permute-start.2 = (f32[3,32768]{1,0:T(4,128)S(1)}, f32[3,32768]{1,0:T(4,128)S(1)}, u32[]{:S(2)}, u32[]{:S(2)}) collective-permute-start(f32[3,32768]{1,0:T(4,128)S(1)} %fusion.234), channel_id=1, source_target_pairs={{0,1},{1,2},{2,3},{3,4},{4,5},{5,6},{6,7},{7,8},{8,9},{9,10},{10,1... | collective-permute-start | bytes 1179656 | tf_op jit(solution)/shard_map/ppermute | solution.py:18
  17.8 23.0 %collective-permute-start.3 = (f32[3,32768]{1,0:T(4,128)S(1)}, f32[3,32768]{1,0:T(4,128)}, u32[]{:S(2)}, u32[]{:S(2)}) collective-permute-start(f32[3,32768]{1,0:T(4,128)S(1)} %fusion.228), channel_id=1, source_target_pairs={{0,2},{1,3},{2,4},{3,5},{4,6},{5,7},{6,8},{7,9},{8,10},{9,11},{10,... | collective-permute-start | bytes 1179656 | tf_op jit(solution)/shard_map/ppermute | solution.py:18
  64.1 14.0 %collective-permute-start.5 = (f32[3,32768]{1,0:T(4,128)S(1)}, f32[3,32768]{1,0:T(4,128)S(1)}, u32[]{:S(2)}, u32[]{:S(2)}) collective-permute-start(f32[3,32768]{1,0:T(4,128)S(1)} %fusion.239), channel_id=1, source_target_pairs={{0,126},{1,127},{2,0},{3,1},{4,2},{5,3},{6,4},{7,5},{8,6},{9,7},{1... | collective-permute-start | bytes 1179656 | tf_op jit(solution)/shard_map/ppermute | solution.py:18
  64.2 13.9 %collective-permute-start.6 = (f32[3,32768]{1,0:T(4,128)S(1)}, f32[3,32768]{1,0:T(4,128)S(1)}, u32[]{:S(2)}, u32[]{:S(2)}) collective-permute-start(f32[3,32768]{1,0:T(4,128)S(1)} %fusion.233), channel_id=1, source_target_pairs={{0,1},{1,2},{2,3},{3,4},{4,5},{5,6},{6,7},{7,8},{8,9},{9,10},{10,1... | collective-permute-start | bytes 1179656 | tf_op jit(solution)/shard_map/ppermute | solution.py:18
  64.3 24.6 %collective-permute-start.7 = (f32[3,32768]{1,0:T(4,128)S(1)}, f32[3,32768]{1,0:T(4,128)S(1)}, u32[]{:S(2)}, u32[]{:S(2)}) collective-permute-start(f32[3,32768]{1,0:T(4,128)S(1)} %fusion.227), channel_id=1, source_target_pairs={{0,2},{1,3},{2,4},{3,5},{4,6},{5,7},{6,8},{7,9},{8,10},{9,11},{10,... | collective-permute-start | bytes 1179656 | tf_op jit(solution)/shard_map/ppermute | solution.py:18
  65.7 24.0 %collective-permute-start.4 = (f32[3,32768]{1,0:T(4,128)S(1)}, f32[3,32768]{1,0:T(4,128)}, u32[]{:S(2)}, u32[]{:S(2)}) collective-permute-start(f32[3,32768]{1,0:T(4,128)S(1)} %fusion.245), channel_id=1, source_target_pairs={{0,127},{1,0},{2,1},{3,2},{4,3},{5,4},{6,5},{7,6},{8,7},{9,8},{10,... | collective-permute-start | bytes 1179656 | tf_op jit(solution)/shard_map/ppermute | solution.py:18
  78.1 10.7 %copy-start.34 = (f32[3,32768]{1,0:T(4,128)}, f32[3,32768]{1,0:T(4,128)S(1)}, u32[]{:S(2)}) copy-start(f32[3,32768]{1,0:T(4,128)S(1)} %collective-permute-done.5) | copy-start | bytes 1179652
  78.1 10.7 %copy-start.37 = (f32[3,32768]{1,0:T(4,128)}, f32[3,32768]{1,0:T(4,128)S(1)}, u32[]{:S(2)}) copy-start(f32[3,32768]{1,0:T(4,128)S(1)} %collective-permute-done.6) | copy-start | bytes 1179652
  109.5 2.2 copy-start.7
  114.7 11.1 %collective-permute-start.10 = (f32[3,32768]{1,0:T(4,128)S(1)}, f32[3,32768]{1,0:T(4,128)S(1)}, u32[]{:S(2)}, u32[]{:S(2)}) collective-permute-start(f32[3,32768]{1,0:T(4,128)S(1)} %fusion.232), channel_id=1, source_target_pairs={{0,1},{1,2},{2,3},{3,4},{4,5},{5,6},{6,7},{7,8},{8,9},{9,10},{10,1... | collective-permute-start | bytes 1179656 | tf_op jit(solution)/shard_map/ppermute | solution.py:18
  114.8 20.7 %collective-permute-start.11 = (f32[3,32768]{1,0:T(4,128)S(1)}, f32[3,32768]{1,0:T(4,128)S(1)}, u32[]{:S(2)}, u32[]{:S(2)}) collective-permute-start(f32[3,32768]{1,0:T(4,128)S(1)} %fusion.226), channel_id=1, source_target_pairs={{0,2},{1,3},{2,4},{3,5},{4,6},{5,7},{6,8},{7,9},{8,10},{9,11},{10,... | collective-permute-start | bytes 1179656 | tf_op jit(solution)/shard_map/ppermute | solution.py:18
  114.9 20.6 %collective-permute-start.9 = (f32[3,32768]{1,0:T(4,128)S(1)}, f32[3,32768]{1,0:T(4,128)S(1)}, u32[]{:S(2)}, u32[]{:S(2)}) collective-permute-start(f32[3,32768]{1,0:T(4,128)S(1)} %fusion.238), channel_id=1, source_target_pairs={{0,126},{1,127},{2,0},{3,1},{4,2},{5,3},{6,4},{7,5},{8,6},{9,7},{1... | collective-permute-start | bytes 1179656 | tf_op jit(solution)/shard_map/ppermute | solution.py:18
  121.8 15.4 %collective-permute-start.8 = (f32[3,32768]{1,0:T(4,128)S(1)}, f32[3,32768]{1,0:T(4,128)}, u32[]{:S(2)}, u32[]{:S(2)}) collective-permute-start(f32[3,32768]{1,0:T(4,128)S(1)} %fusion.244), channel_id=1, source_target_pairs={{0,127},{1,0},{2,1},{3,2},{4,3},{5,4},{6,5},{7,6},{8,7},{9,8},{10,... | collective-permute-start | bytes 1179656 | tf_op jit(solution)/shard_map/ppermute | solution.py:18
  125.9 9.7 %copy-start.35 = (f32[3,32768]{1,0:T(4,128)}, f32[3,32768]{1,0:T(4,128)S(1)}, u32[]{:S(2)}) copy-start(f32[3,32768]{1,0:T(4,128)S(1)} %collective-permute-done.10) | copy-start | bytes 1179652
  157.0 2.2 copy-start.8
  157.0 2.2 copy-start.16
  160.4 34.9 %copy-start.24 = (f32[4,32768]{1,0:T(4,128)S(1)}, f32[4,32768]{1,0:T(4,128)}, u32[]{:S(2)}) copy-start(f32[4,32768]{1,0:T(4,128)} %get-tuple-element.20) | copy-start | bytes 1572868
  163.5 17.5 %collective-permute-start.13 = (f32[3,32768]{1,0:T(4,128)S(1)}, f32[3,32768]{1,0:T(4,128)S(1)}, u32[]{:S(2)}, u32[]{:S(2)}) collective-permute-start(f32[3,32768]{1,0:T(4,128)S(1)} %fusion.237), channel_id=1, source_target_pairs={{0,126},{1,127},{2,0},{3,1},{4,2},{5,3},{6,4},{7,5},{8,6},{9,7},{1... | collective-permute-start | bytes 1179656 | tf_op jit(solution)/shard_map/ppermute | solution.py:18
  173.0 11.1 %collective-permute-start.14 = (f32[3,32768]{1,0:T(4,128)S(1)}, f32[3,32768]{1,0:T(4,128)S(1)}, u32[]{:S(2)}, u32[]{:S(2)}) collective-permute-start(f32[3,32768]{1,0:T(4,128)S(1)} %fusion.231), channel_id=1, source_target_pairs={{0,1},{1,2},{2,3},{3,4},{4,5},{5,6},{6,7},{7,8},{8,9},{9,10},{10,1... | collective-permute-start | bytes 1179656 | tf_op jit(solution)/shard_map/ppermute | solution.py:18
  173.0 20.6 %collective-permute-start.15 = (f32[3,32768]{1,0:T(4,128)S(1)}, f32[3,32768]{1,0:T(4,128)S(1)}, u32[]{:S(2)}, u32[]{:S(2)}) collective-permute-start(f32[3,32768]{1,0:T(4,128)S(1)} %fusion.225), channel_id=1, source_target_pairs={{0,2},{1,3},{2,4},{3,5},{4,6},{5,7},{6,8},{7,9},{8,10},{9,11},{10,... | collective-permute-start | bytes 1179656 | tf_op jit(solution)/shard_map/ppermute | solution.py:18
  173.0 20.6 %collective-permute-start.12 = (f32[3,32768]{1,0:T(4,128)S(1)}, f32[3,32768]{1,0:T(4,128)S(1)}, u32[]{:S(2)}, u32[]{:S(2)}) collective-permute-start(f32[3,32768]{1,0:T(4,128)S(1)} %fusion.243), channel_id=1, source_target_pairs={{0,127},{1,0},{2,1},{3,2},{4,3},{5,4},{6,5},{7,6},{8,7},{9,8},{10,... | collective-permute-start | bytes 1179656 | tf_op jit(solution)/shard_map/ppermute | solution.py:18
  181.0 12.7 %copy-start.33 = (f32[3,32768]{1,0:T(4,128)}, f32[3,32768]{1,0:T(4,128)S(1)}, u32[]{:S(2)}) copy-start(f32[3,32768]{1,0:T(4,128)S(1)} %collective-permute-done.13) | copy-start | bytes 1179652
  184.0 9.6 %copy-start.36 = (f32[3,32768]{1,0:T(4,128)}, f32[3,32768]{1,0:T(4,128)S(1)}, u32[]{:S(2)}) copy-start(f32[3,32768]{1,0:T(4,128)S(1)} %collective-permute-done.14) | copy-start | bytes 1179652
  217.1 8.3 %copy-start.26 = (f32[512,128]{1,0:T(8,128)S(1)}, f32[512,128]{1,0:T(8,128)}, u32[]{:S(2)}) copy-start(f32[512,128]{1,0:T(8,128)} %param.8) | copy-start | bytes 786436
  218.5 7.7 %copy-start.27 = (f32[512,128]{1,0:T(8,128)S(1)}, f32[512,128]{1,0:T(8,128)}, u32[]{:S(2)}) copy-start(f32[512,128]{1,0:T(8,128)} %param.7) | copy-start | bytes 786436
  218.5 8.5 %copy-start.10 = (f32[4,256,128]{1,2,0:T(8,128)S(1)}, f32[4,256,128]{1,2,0:T(8,128)}, u32[]{:S(2)}) copy-start(f32[4,256,128]{1,2,0:T(8,128)} %copy-done.9) | copy-start | bytes 1572868
  220.0 8.1 %copy-start.12 = (f32[4,256,128]{1,2,0:T(8,128)S(1)}, f32[4,256,128]{1,2,0:T(8,128)}, u32[]{:S(2)}) copy-start(f32[4,256,128]{1,2,0:T(8,128)} %copy-done.11) | copy-start | bytes 1572868
  221.4 7.6 %copy-start.14 = (f32[4,256,128]{1,2,0:T(8,128)S(1)}, f32[4,256,128]{1,2,0:T(8,128)}, u32[]{:S(2)}) copy-start(f32[4,256,128]{1,2,0:T(8,128)} %copy-done.13) | copy-start | bytes 1572868
  223.1 13.7 %collective-permute-start.17 = (f32[3,32768]{1,0:T(4,128)}, f32[3,32768]{1,0:T(4,128)}, u32[]{:S(2)}, u32[]{:S(2)}) collective-permute-start(f32[3,32768]{1,0:T(4,128)} %fusion.236), channel_id=1, source_target_pairs={{0,126},{1,127},{2,0},{3,1},{4,2},{5,3},{6,4},{7,5},{8,6},{9,7},{1... | collective-permute-start | bytes 1179656 | tf_op jit(solution)/shard_map/ppermute | solution.py:18
  223.1 13.7 %collective-permute-start.18 = (f32[3,32768]{1,0:T(4,128)}, f32[3,32768]{1,0:T(4,128)}, u32[]{:S(2)}, u32[]{:S(2)}) collective-permute-start(f32[3,32768]{1,0:T(4,128)} %fusion.230), channel_id=1, source_target_pairs={{0,1},{1,2},{2,3},{3,4},{4,5},{5,6},{6,7},{7,8},{8,9},{9,10},{10,1... | collective-permute-start | bytes 1179656 | tf_op jit(solution)/shard_map/ppermute | solution.py:18
  224.8 23.3 %collective-permute-start.19 = (f32[3,32768]{1,0:T(4,128)}, f32[3,32768]{1,0:T(4,128)}, u32[]{:S(2)}, u32[]{:S(2)}) collective-permute-start(f32[3,32768]{1,0:T(4,128)} %fusion.224), channel_id=1, source_target_pairs={{0,2},{1,3},{2,4},{3,5},{4,6},{5,7},{6,8},{7,9},{8,10},{9,11},{10,... | collective-permute-start | bytes 1179656 | tf_op jit(solution)/shard_map/ppermute | solution.py:18
  224.8 23.3 %collective-permute-start.16 = (f32[3,32768]{1,0:T(4,128)}, f32[3,32768]{1,0:T(4,128)}, u32[]{:S(2)}, u32[]{:S(2)}) collective-permute-start(f32[3,32768]{1,0:T(4,128)} %fusion.242), channel_id=1, source_target_pairs={{0,127},{1,0},{2,1},{3,2},{4,3},{5,4},{6,5},{7,6},{8,7},{9,8},{10,... | collective-permute-start | bytes 1179656 | tf_op jit(solution)/shard_map/ppermute | solution.py:18
  267.9 2.5 copy-start.18
  267.9 2.5 copy-start.19
  267.9 2.4 copy-start.20
  268.0 2.4 copy-start.21
  272.9 5.5 %copy-start.25 = (f32[512,256]{0,1:T(8,128)S(1)}, f32[512,256]{0,1:T(8,128)}, u32[]{:S(2)}) copy-start(f32[512,256]{0,1:T(8,128)} %get-tuple-element.19) | copy-start | bytes 1572868
  274.8 8.2 %collective-permute-start.20 = (f32[3,16384]{1,0:T(4,128)S(1)}, f32[3,16384]{1,0:T(4,128)S(1)}, u32[]{:S(2)}, u32[]{:S(2)}) collective-permute-start(f32[3,16384]{1,0:T(4,128)S(1)} %fusion.241), channel_id=1, source_target_pairs={{0,127},{1,0},{2,1},{3,2},{4,3},{5,4},{6,5},{7,6},{8,7},{9,8},{10,... | collective-permute-start | bytes 589832 | tf_op jit(solution)/shard_map/ppermute | solution.py:18
  274.9 8.1 %collective-permute-start.21 = (f32[3,16384]{1,0:T(4,128)S(1)}, f32[3,16384]{1,0:T(4,128)S(1)}, u32[]{:S(2)}, u32[]{:S(2)}) collective-permute-start(f32[3,16384]{1,0:T(4,128)S(1)} %fusion.235), channel_id=1, source_target_pairs={{0,126},{1,127},{2,0},{3,1},{4,2},{5,3},{6,4},{7,5},{8,6},{9,7},{1... | collective-permute-start | bytes 589832 | tf_op jit(solution)/shard_map/ppermute | solution.py:18
  275.0 8.0 %collective-permute-start.22 = (f32[3,16384]{1,0:T(4,128)S(1)}, f32[3,16384]{1,0:T(4,128)S(1)}, u32[]{:S(2)}, u32[]{:S(2)}) collective-permute-start(f32[3,16384]{1,0:T(4,128)S(1)} %fusion.229), channel_id=1, source_target_pairs={{0,1},{1,2},{2,3},{3,4},{4,5},{5,6},{6,7},{7,8},{8,9},{9,10},{10,1... | collective-permute-start | bytes 589832 | tf_op jit(solution)/shard_map/ppermute | solution.py:18
  277.0 14.6 %collective-permute-start.23 = (f32[3,16384]{1,0:T(4,128)S(1)}, f32[3,16384]{1,0:T(4,128)}, u32[]{:S(2)}, u32[]{:S(2)}) collective-permute-start(f32[3,16384]{1,0:T(4,128)S(1)} %fusion.223), channel_id=1, source_target_pairs={{0,2},{1,3},{2,4},{3,5},{4,6},{5,7},{6,8},{7,9},{8,10},{9,11},{10,... | collective-permute-start | bytes 589832 | tf_op jit(solution)/shard_map/ppermute | solution.py:18
  329.9 13.1 %all-to-all-start.1 = ((f32[64,1,169]{2,1,0:T(1,128)}), f32[64,1,169]{2,1,0:T(1,128)S(1)}, u32[]{:S(2)}, u32[]{:S(2)}) async-start(f32[64,1,169]{2,1,0:T(1,128)} %reshape.342), calls=%async_computation.1 | async-start | bytes 131072 | tf_op jit(solution)/shard_map/all_to_all | solution.py:36
  345.1 13.4 %all-to-all-start.2 = ((f32[64,1,169]{2,1,0:T(1,128)}), f32[64,1,169]{2,1,0:T(1,128)S(1)}, u32[]{:S(2)}, u32[]{:S(2)}) async-start(f32[64,1,169]{2,1,0:T(1,128)} %reshape.344), calls=%async_computation.2 | async-start | bytes 131072 | tf_op jit(solution)/shard_map/all_to_all | solution.py:46
  375.5 6.1 %copy-start.43 = (f32[512,128]{1,0:T(8,128)S(1)}, f32[512,128]{1,0:T(8,128)}, u32[]{:S(2)}) copy-start(f32[512,128]{1,0:T(8,128)} %param.6) | copy-start | bytes 786436
  (27 other events, 32.3 us)
where the time goes:
time: 390 us; the launch traced here: 383 us
  waiting for transfers between devices  119 us (31%)
  local copies, waits for them, and re-layouts  106 us (27%)
  matrix products  79.3 us (20%)
  starting transfers between devices  47.2 us (12%)
  other arithmetic  18.1 us (5%)
  blocking collectives  9.67 us (2%)
    ppermute x24, waiting for transfers between devices, from_behind(): lax.ppermute(shard, axis, [(i, (i + by) % peers) for i in range(peers)])  103 us
    concatenate x6, local copies, waits for them, and re-layouts, apply_blocks(): ghost_table = jnp.concatenate(pieces, axis=0)  65.5 us
    ppermute x24, starting transfers between devices, from_behind(): lax.ppermute(shard, axis, [(i, (i + by) % peers) for i in range(peers)])  37.7 us
    dot_general x36, matrix products, apply_blocks(): jnp.dot(chooser, ghost_table, precision=highest)  27.6 us
    dot_general x36, matrix products, apply_blocks(): jnp.einsum('icb,ibw->icw', block_vals[:, slot_index], picked, precision=h...  22.8 us
    dot_general x24, matrix products, apply_blocks(): outgoing = jnp.dot(chooser, flat_rows, precision=highest)  19 us
    unnamed x128, local copies, waits for them, and re-layouts  15.8 us
    another operation x16, local copies, waits for them, and re-layouts, shards(): basis_stack = jnp.stack(p_basis + r_basis)  14.9 us
  transfers between devices with their start and end apart: 26, of which 17 were waited for; matrix products, arithmetic and copies ran while one was open for 3% of the time, Pallas kernels for 0%

commit v1 on v0

v1 whole, which is shorter than its diff:
```python
import functools

import jax
import jax.numpy as jnp
from jax import lax
from jax.experimental import pallas as pl
from jax.experimental.pallas import tpu as pltpu
from jax.sharding import PartitionSpec as P

MESH = pl.DeviceIdType.MESH
STEPS = 6
BASIS = 13
BLOCK = 128
NB = 4
SLOTS = 6
CAP = 3
OFFSETS = (1, 2, -1, -2)
NEAR = 8
MOMENTS = 40
PP, PR, RR = 0, 13, 24
center_value = 4.5
half_range = 4.5


def split_two(value):
    high = value.astype(jnp.bfloat16)
    low = (value - high.astype(jnp.float32)).astype(jnp.bfloat16)
    return high, low


def kernel(
    peers,
    start_hbm, resid_hbm, direc_hbm, send_ref, cols_ref, vals_hbm,
    point_hbm, newres_hbm, newdir_hbm,
    p_basis, r_basis, start_v, vals_v, mats, diag, table,
    stage_p, stage_r, ghost_p, ghost_r,
    moments, near_buf, near_sum, far_buf, total, late, late_near, late_sum, late_far,
    gram, coefs, outs,
    load_sem, out_sem, send_p, recv_p, send_r, recv_r,
    near_send, near_recv, far_send, far_recv, lnear_send, lnear_recv, lfar_send, lfar_recv,
):
    me = lax.axis_index("dom")
    low = lax.rem(me, NEAR)
    base = me - low
    high = me // NEAR
    far_count = peers // NEAR

    loads = [
        pltpu.make_async_copy(direc_hbm, p_basis.at[0], load_sem.at[0]),
        pltpu.make_async_copy(resid_hbm, r_basis.at[0], load_sem.at[1]),
        pltpu.make_async_copy(vals_hbm, vals_v, load_sem.at[2]),
        pltpu.make_async_copy(start_hbm, start_v, load_sem.at[3]),
    ]
    for load in loads:
        load.start()

    near_peers = [(base + lax.rem(low + d, NEAR), lax.rem(low + d, NEAR)) for d in range(1, NEAR)]
    far_peers = [
        (lax.rem(high + d, far_count) * NEAR + low, lax.rem(high + d, far_count))
        for d in range(1, far_count)
    ]
    barrier = pltpu.get_barrier_semaphore()
    for offset in OFFSETS:
        pl.semaphore_signal(
            barrier, inc=1, device_id=(lax.rem(me - offset + peers, peers),), device_id_type=MESH
        )
    for device, _ in near_peers + far_peers:
        pl.semaphore_signal(barrier, inc=1, device_id=(device,), device_id_type=MESH)
    pl.semaphore_wait(barrier, len(OFFSETS) + len(near_peers) + len(far_peers))

    def exchange(stage, ghost, sends, recvs, parity):
        return [
            pltpu.make_async_remote_copy(
                src_ref=stage.at[m],
                dst_ref=ghost.at[parity, m],
                send_sem=sends.at[m],
                recv_sem=recvs.at[parity, m],
                device_id=(lax.rem(me - offset + peers, peers),),
                device_id_type=MESH,
            )
            for m, offset in enumerate(OFFSETS)
        ]

    def send(basis, step, stage, ghost, sends, recvs):
        copies = exchange(stage, ghost, sends, recvs, lax.rem(step, 2))
        for m in (1, 3, 0, 2):
            for e in range(CAP):
                stage[m, e] = basis[step, send_ref[0, m, e]]
            copies[m].start()

    def own_table(basis, step):
        hi, lo = split_two(basis[step])
        table[0:NB, :, 0:BLOCK] = hi
        table[0:NB, :, BLOCK:] = lo

    def advance(basis, step, stage, ghost, sends, recvs):
        own_table(basis, step)
        parity = lax.rem(step, 2)
        copies = exchange(stage, ghost, sends, recvs, parity)
        for m in (0, 2, 1, 3):
            copies[m].wait_recv()
            hi, lo = split_two(ghost[parity, m])
            at = NB + m * CAP
            table[at : at + CAP, :, 0:BLOCK] = hi
            table[at : at + CAP, :, BLOCK:] = lo
        for copy in copies:
            copy.wait_send()
        for i in range(NB):
            parts = None
            for k in range(0, SLOTS, 2):
                pair = jnp.concatenate([table[cols_ref[i, k]], table[cols_ref[i, k + 1]]], axis=0)
                term = jnp.dot(
                    mats[i, :, k * BLOCK : (k + 2) * BLOCK], pair, preferred_element_type=jnp.float32
                )
                parts = term if parts is None else parts + term
            image = parts[0:BLOCK, 0:BLOCK] + (parts[0:BLOCK, BLOCK:] + parts[BLOCK:, 0:BLOCK])
            basis[step + 1, i] = image + diag[i] * basis[step, i]

    def dot_of(one, two):
        return jnp.sum(jnp.sum((one * two).reshape(-1, 8, BLOCK), axis=0), axis=0, keepdims=True)

    def dots(target, pairs):
        for row, one, two in pairs:
            target[pl.ds(row, 1), :] = dot_of(one, two)

    def level(step):
        p_new, p_old = p_basis[step], p_basis[step - 1]
        r_new, r_old = r_basis[step], r_basis[step - 1]
        dots(
            moments,
            [
                (PP + 2 * step, p_new, p_new),
                (PP + 2 * step - 1, p_new, p_old),
                (PR + 2 * step, p_new, r_new),
                (PR + 2 * step - 1, p_new, r_old),
                (RR + 2 * step, r_new, r_new),
                (RR + 2 * step - 1, r_new, r_old),
            ],
        )

    def group_copy(source, target, sends, recvs, n, device, slot):
        return pltpu.make_async_remote_copy(
            src_ref=source,
            dst_ref=target.at[slot],
            send_sem=sends.at[n],
            recv_sem=recvs.at[slot],
            device_id=(device,),
            device_id_type=MESH,
        )

    def group_start(source, target, sends, recvs, mine, group):
        for n, (device, _) in enumerate(group):
            group_copy(source, target, sends, recvs, n, device, mine).start()

    def group_sum(source, target, sends, recvs, mine, group):
        for n, (device, slot) in enumerate(group):
            group_copy(source, target, sends, recvs, n, device, slot).wait()
        target[mine] = source[...]
        return jnp.sum(target[...], axis=0)

    loads[0].wait()
    send(p_basis, 0, stage_p, ghost_p, send_p, recv_p)
    loads[1].wait()
    send(r_basis, 0, stage_r, ghost_r, send_r, recv_r)
    loads[2].wait()

    rows = lax.broadcasted_iota(jnp.int32, (BLOCK, BLOCK), 0)
    lanes = lax.broadcasted_iota(jnp.int32, (BLOCK, BLOCK), 1)
    for i in range(NB):
        for k in range(SLOTS):
            values = vals_v[i, k]
            if k == 0:
                on_diag = jnp.where(rows == lanes, values, 0.0)
                column = (jnp.sum(on_diag, axis=1, keepdims=True) - center_value) / half_range
                diag[i] = jnp.broadcast_to(column, (BLOCK, BLOCK))
                values = jnp.where(rows == lanes, 0.0, values)
            hi, lo = split_two(values * (1.0 / half_range))
            mats[i, 0:BLOCK, k * BLOCK : (k + 1) * BLOCK] = hi
            mats[i, BLOCK:, k * BLOCK : (k + 1) * BLOCK] = lo
    moments[...] = jnp.zeros_like(moments)
    late[...] = jnp.zeros_like(late)
    gram[...] = jnp.zeros_like(gram)
    dots(
        moments,
        [
            (PP, p_basis[0], p_basis[0]),
            (PR, p_basis[0], r_basis[0]),
            (RR, r_basis[0], r_basis[0]),
        ],
    )

    def step_body(step, carry):
        advance(p_basis, step, stage_p, ghost_p, send_p, recv_p)
        send(p_basis, step + 1, stage_p, ghost_p, send_p, recv_p)
        advance(r_basis, step, stage_r, ghost_r, send_r, recv_r)

        @pl.when(step < STEPS - 2)
        def _():
            send(r_basis, step + 1, stage_r, ghost_r, send_r, recv_r)

        level(step + 1)
        return carry

    lax.fori_loop(0, STEPS - 1, step_body, 0)

    group_start(moments, near_buf, near_send, near_recv, low, near_peers)
    near_sum[...] = group_sum(moments, near_buf, near_send, near_recv, low, near_peers)
    group_start(near_sum, far_buf, far_send, far_recv, high, far_peers)

    advance(p_basis, STEPS - 1, stage_p, ghost_p, send_p, recv_p)
    p_last = p_basis[STEPS]
    dots(
        late,
        [
            (0, p_last, p_basis[STEPS - 1]),
            (1, p_last, p_last),
            (2, p_last, r_basis[STEPS - 1]),
        ],
    )
    group_start(late, late_near, lnear_send, lnear_recv, low, near_peers)
    late_sum[...] = group_sum(late, late_near, lnear_send, lnear_recv, low, near_peers)
    group_start(late_sum, late_far, lfar_send, lfar_recv, high, far_peers)
    loads[3].wait()
    total[...] = group_sum(near_sum, far_buf, far_send, far_recv, high, far_peers)
    last = group_sum(late_sum, late_far, lfar_send, lfar_recv, high, far_peers)
    total[PP + 11 : PP + 13, :] = last[0:2]
    pr_last = last[2:3]

    def pr_rows(first, count):
        wanted = min(first + count, 11) - first
        part = total[PR + first : PR + first + wanted, :]
        return part if wanted == count else jnp.concatenate([part, pr_last], axis=0)

    for b in range(STEPS + 1):
        gram[b, 0 : STEPS + 1, :] = total[PP + b : PP + b + STEPS + 1, :]
        gram[b, STEPS + 1 : BASIS, :] = pr_rows(b, STEPS)
    for b in range(STEPS):
        gram[STEPS + 1 + b, 0 : STEPS + 1, :] = pr_rows(b, STEPS + 1)
        gram[STEPS + 1 + b, STEPS + 1 : BASIS, :] = total[RR + b : RR + b + STEPS, :]

    places = lax.broadcasted_iota(jnp.int32, (16, BLOCK), 0)
    active = (places < STEPS) | ((places > STEPS) & (places < BASIS - 1))

    def times_gram(vector):
        sums = [gram[b] * vector[b : b + 1, :] for b in range(BASIS)]
        while len(sums) > 1:
            sums = [a + b for a, b in zip(sums[::2], sums[1::2])] + (
                [sums[-1]] if len(sums) % 2 else []
            )
        return sums[0]

    def inner(one, two):
        return jnp.sum(one * two, axis=0, keepdims=True)

    point_c = jnp.zeros((16, BLOCK), jnp.float32)
    resid_c = jnp.where(places == STEPS + 1, 1.0, 0.0).astype(jnp.float32)
    direc_c = jnp.where(places == 0, 1.0, 0.0).astype(jnp.float32)
    current = inner(resid_c, times_gram(resid_c))
    for _ in range(STEPS):
        held = jnp.where(active, direc_c, 0.0)
        shifted = jnp.concatenate([jnp.zeros((1, BLOCK), jnp.float32), held[0:15]], axis=0)
        moved = center_value * held + half_range * shifted
        alpha = current / inner(direc_c, times_gram(moved))
        point_c = point_c + alpha * direc_c
        resid_c = resid_c - alpha * moved
        following = inner(resid_c, times_gram(resid_c))
        direc_c = resid_c + (following / current) * direc_c
        current = following
    coefs[0] = point_c
    coefs[1] = resid_c
    coefs[2] = direc_c

    copies = []
    for i in range(NB):
        def combine(chunk, carry):
            at = pl.ds(chunk * 32, 32)
            sums = [start_v[i, at, :], None, None]
            for a in range(BASIS):
                piece = p_basis[a, i, at, :] if a <= STEPS else r_basis[a - STEPS - 1, i, at, :]
                for o in range(3):
                    term = coefs[o, a : a + 1, :] * piece
                    sums[o] = term if sums[o] is None else sums[o] + term
            for o in range(3):
                outs[o, i, at, :] = sums[o]
            return carry

        lax.fori_loop(0, BLOCK // 32, combine, 0)
        for o, target in enumerate((point_hbm, newres_hbm, newdir_hbm)):
            copy = pltpu.make_async_copy(outs.at[o, i], target.at[i], out_sem.at[o, i])
            copy.start()
            copies.append(copy)
    for copy in copies:
        copy.wait()


def shards(start_point, residual, direction, send_list, block_cols, block_vals, *, peers):
    far_count = peers // NEAR
    blocked = (NB, BLOCK, BLOCK)
    any_space = pl.BlockSpec(memory_space=pl.ANY)
    scalars = pl.BlockSpec(memory_space=pltpu.SMEM)
    f32 = jnp.float32
    dma = pltpu.SemaphoreType.DMA
    results = pl.pallas_call(
        functools.partial(kernel, peers),
        out_shape=[jax.ShapeDtypeStruct(blocked, f32)] * 3,
        in_specs=[any_space, any_space, any_space, scalars, scalars, any_space],
        out_specs=[any_space] * 3,
        scratch_shapes=[
            pltpu.VMEM((STEPS + 1, *blocked), f32),
            pltpu.VMEM((STEPS, *blocked), f32),
            pltpu.VMEM(blocked, f32),
            pltpu.VMEM((NB, SLOTS, BLOCK, BLOCK), f32),
            pltpu.VMEM((NB, 2 * BLOCK, SLOTS * BLOCK), jnp.bfloat16),
            pltpu.VMEM(blocked, f32),
            pltpu.VMEM((NB + 4 * CAP, BLOCK, 2 * BLOCK), jnp.bfloat16),
            pltpu.VMEM((4, CAP, BLOCK, BLOCK), f32),
            pltpu.VMEM((4, CAP, BLOCK, BLOCK), f32),
            pltpu.VMEM((2, 4, CAP, BLOCK, BLOCK), f32),
            pltpu.VMEM((2, 4, CAP, BLOCK, BLOCK), f32),
            pltpu.VMEM((MOMENTS, BLOCK), f32),
            pltpu.VMEM((NEAR, MOMENTS, BLOCK), f32),
            pltpu.VMEM((MOMENTS, BLOCK), f32),
            pltpu.VMEM((far_count, MOMENTS, BLOCK), f32),
            pltpu.VMEM((MOMENTS, BLOCK), f32),
            pltpu.VMEM((8, BLOCK), f32),
            pltpu.VMEM((NEAR, 8, BLOCK), f32),
            pltpu.VMEM((8, BLOCK), f32),
            pltpu.VMEM((far_count, 8, BLOCK), f32),
            pltpu.VMEM((BASIS, 16, BLOCK), f32),
            pltpu.VMEM((3, 16, BLOCK), f32),
            pltpu.VMEM((3, *blocked), f32),
            dma((4,)),
            dma((3, NB)),
            dma((4,)),
            dma((2, 4)),
            dma((4,)),
            dma((2, 4)),
            dma((NEAR - 1,)),
            dma((NEAR,)),
            dma((far_count - 1,)),
            dma((far_count,)),
            dma((NEAR - 1,)),
            dma((NEAR,)),
            dma((far_count - 1,)),
            dma((far_count,)),
        ],
        compiler_params=pltpu.CompilerParams(
            collective_id=0, has_side_effects=True, vmem_limit_bytes=56 * 1024 * 1024
        ),
        name="cg_steps",
    )(
        start_point.reshape(blocked),
        residual.reshape(blocked),
        direction.reshape(blocked),
        send_list,
        block_cols,
        block_vals,
    )
    return tuple(result.reshape(NB * BLOCK, BLOCK) for result in results)


def solution(mesh):
    return jax.shard_map(
        functools.partial(shards, peers=mesh.shape["dom"]),
        mesh=mesh,
        in_specs=(
            P("dom", None),
            P("dom", None),
            P("dom", None),
            P("dom", None, None),
            P("dom", None),
            P("dom", None, None, None),
        ),
        out_specs=(P("dom", None), P("dom", None), P("dom", None)),
        check_vma=False,
    )
```

time: 390 us -> 104 us (0.27); the launches traced: 383 us -> 103 us
  waiting for transfers between devices: 119 us -> 0 us
  local copies, waits for them, and re-layouts: 106 us -> 6.35 us
  Pallas kernels: 0 us -> 96.4 us
  matrix products: 79.3 us -> 0 us
  starting transfers between devices: 47.2 us -> 0 us
  other arithmetic: 18.1 us -> 0 us
  blocking collectives: 9.67 us -> 0 us
    ppermute x24 -> x0, waiting for transfers between devices: 103 us -> none  [from_behind(): lax.ppermute(shard, axis, [(i, (i + by) % peers) for i in range(peers)])]
    pallas_call x0 -> x1, Pallas kernels: none -> 96.4 us  [shards(): pl.pallas_call(functools.partial(kernel, peers), out_shape=[jax.ShapeDtyp...]
    dot_general x103 -> x0, matrix products: 79.3 us -> none  [the longest x36 27.6 us: apply_blocks(): jnp.dot(chooser, ghost_table, precision=highest)]
    concatenate x7 -> x0, local copies, waits for them, and re-layouts: 65.7 us -> none  [the longest x6 65.5 us: apply_blocks(): ghost_table = jnp.concatenate(pieces, axis=0)]
    ppermute x24 -> x0, starting transfers between devices: 37.7 us -> none  [from_behind(): lax.ppermute(shard, axis, [(i, (i + by) % peers) for i in range(peers)])]
    all_to_all x2 -> x0, waiting for transfers between devices: 16.6 us -> none  [the longest x1 8.32 us: sent_to_all(): lax.all_to_all(jnp.broadcast_to(shard[None], (peers, *shard.shape)), axis...]
    another operation x19 -> x0, local copies, waits for them, and re-layouts: 15.9 us -> none  [the longest x16 14.9 us: shards(): basis_stack = jnp.stack(p_basis + r_basis)]
    all_to_all x2 -> x0, blocking collectives: 9.67 us -> none  [the longest x1 6.06 us: sent_to_all(): lax.all_to_all(jnp.broadcast_to(shard[None], (peers, *shard.shape)), axis...]
  transfers between devices with their start and end apart: 26 -> 0, of which waited for: 17 -> 0; matrix products, arithmetic and copies ran while one was open for 3% -> 0% of each run, Pallas kernels for 0% -> 0%
where the time goes in v1:
time: 104 us; the launch traced here: 103 us
  Pallas kernels  96.4 us (93%)
  local copies, waits for them, and re-layouts  6.35 us (6%)
    pallas_call x1, Pallas kernels, shards(): pl.pallas_call(functools.partial(kernel, peers), out_shape=[jax.ShapeDtyp...  96.4 us
    unnamed x4, local copies, waits for them, and re-layouts  6.35 us

profile of v1, /device:TPU:1, one launch (start us, length us, event | category | flops | bytes accessed | tf_op | source)
XLA Modules:
  0.0 103.4 jit_solution(722029153192129782)
XLA Ops:
  0.6 1.3 %copy.9.send_ref = s32[1,4,3]{2,1,0:T(4,128)} copy(s32[1,4,3]{1,0,2:T(1,128)} %param.9) | data formatting | bytes 96 | tf_op args[3]
  2.0 96.4 %cg_steps.1 = (f32[4,128,128]{2,1,0:T(8,128)}, f32[4,128,128]{2,1,0:T(8,128)}, f32[4,128,128]{2,1,0:T(8,128)}) custom-call(f32[4,128,128]{2,1,0:T(8,128)} %bitcast.6, f32[4,128,128]{2,1,0:T(8,128)} %bitcast.7, f32[4,128,128]{2,1,0:T(8,128)} %bitcast.8, s32[1,4,3]{2,1,0:T(4,128)} %copy.9.send_ref, s32[4,6]{1,0:T(4,128)} %cols_ref.1, f32[4,6,128,128]{3,2,1,0:T(8,128)} %vals_hbm.1), custom_call_target="tpu_custom_call" | custom-call | tf_op jit(solution)/shard_map/cg_steps/pallas_call | solution.py:303
  98.4 1.7 %copy.13 = f32[512,128]{1,0:T(8,128)} copy(f32[512,128]{1,0:T(8,128)} %bitcast.11) | data formatting | bytes 524288
  100.0 1.7 %copy.14 = f32[512,128]{1,0:T(8,128)} copy(f32[512,128]{1,0:T(8,128)} %bitcast.10) | data formatting | bytes 524288
  101.7 1.7 %copy.15 = f32[512,128]{1,0:T(8,128)} copy(f32[512,128]{1,0:T(8,128)} %bitcast.9) | data formatting | bytes 524288

commit v2 on v1

--- a/solution.py
+++ b/solution.py
@@ -14,9 +14,11 @@
 NB = 4
 SLOTS = 6
 CAP = 3
-OFFSETS = (1, 2, -1, -2)
+GHOSTS = 14
+X_AT, Y_AT, FAR_AT, SIB_AT = 0, 4, 8, 11
 NEAR = 8
 MOMENTS = 40
+VMEM_GRANT = 24 * 1024 * 1024
 PP, PR, RR = 0, 13, 24
 center_value = 4.5
 half_range = 4.5
@@ -30,13 +32,13 @@
 
 def kernel(
     peers,
-    start_hbm, resid_hbm, direc_hbm, send_ref, cols_ref, vals_hbm,
-    point_hbm, newres_hbm, newdir_hbm,
+    start_hbm, resid_hbm, direc_hbm, send_hbm, cols_hbm, vals_hbm,
+    outs,
     p_basis, r_basis, start_v, vals_v, mats, diag, table,
     stage_p, stage_r, ghost_p, ghost_r,
     moments, near_buf, near_sum, far_buf, total, late, late_near, late_sum, late_far,
-    gram, coefs, outs,
-    load_sem, out_sem, send_p, recv_p, send_r, recv_r,
+    gram, coefs, cols_ref, send_ref, send_vmem, lists_v, lists_s, ghost_map, places,
+    load_sem, list_send, list_recv, send_p, recv_p, send_r, recv_r,
     near_send, near_recv, far_send, far_recv, lnear_send, lnear_recv, lfar_send, lfar_recv,
 ):
     me = lax.axis_index("dom")
@@ -45,13 +47,25 @@
     high = me // NEAR
     far_count = peers // NEAR
 
+    odd = lax.rem(me, 2)
+    sign = 2 * odd - 1
+    x_dev = lax.rem(me + sign + peers, peers)
+    y_dev = lax.rem(me - 2 * sign + peers, peers)
+    w_dev = lax.rem(me + 2 * sign + peers, peers)
+    sibling = me - sign
+
     loads = [
         pltpu.make_async_copy(direc_hbm, p_basis.at[0], load_sem.at[0]),
         pltpu.make_async_copy(resid_hbm, r_basis.at[0], load_sem.at[1]),
         pltpu.make_async_copy(vals_hbm, vals_v, load_sem.at[2]),
         pltpu.make_async_copy(start_hbm, start_v, load_sem.at[3]),
     ]
-    for load in loads:
+    lists = [
+        pltpu.make_async_copy(send_hbm, send_ref, load_sem.at[4]),
+        pltpu.make_async_copy(send_hbm, send_vmem, load_sem.at[5]),
+        pltpu.make_async_copy(cols_hbm, cols_ref, load_sem.at[7]),
+    ]
+    for load in lists + loads:
         load.start()
 
     near_peers = [(base + lax.rem(low + d, NEAR), lax.rem(low + d, NEAR)) for d in range(1, NEAR)]
@@ -60,33 +74,52 @@
         for d in range(1, far_count)
     ]
     barrier = pltpu.get_barrier_semaphore()
-    for offset in OFFSETS:
-        pl.semaphore_signal(
-            barrier, inc=1, device_id=(lax.rem(me - offset + peers, peers),), device_id_type=MESH
-        )
+    for device in (x_dev, y_dev, w_dev, sibling):
+        pl.semaphore_signal(barrier, inc=1, device_id=(device,), device_id_type=MESH)
     for device, _ in near_peers + far_peers:
         pl.semaphore_signal(barrier, inc=1, device_id=(device,), device_id_type=MESH)
-    pl.semaphore_wait(barrier, len(OFFSETS) + len(near_peers) + len(far_peers))
-
-    def exchange(stage, ghost, sends, recvs, parity):
+
+    def remote(source, ghost, sends, recvs, parity, at, count, n, device):
+        return pltpu.make_async_remote_copy(
+            src_ref=source,
+            dst_ref=ghost.at[parity, pl.ds(at, count)],
+            send_sem=sends.at[n],
+            recv_sem=recvs.at[parity, n],
+            device_id=(device,),
+            device_id_type=MESH,
+        )
+
+    def direct(basis, step, stage, ghost, sends, recvs):
+        common = (ghost, sends, recvs, lax.rem(step, 2))
         return [
-            pltpu.make_async_remote_copy(
-                src_ref=stage.at[m],
-                dst_ref=ghost.at[parity, m],
-                send_sem=sends.at[m],
-                recv_sem=recvs.at[parity, m],
-                device_id=(lax.rem(me - offset + peers, peers),),
-                device_id_type=MESH,
-            )
-            for m, offset in enumerate(OFFSETS)
+            remote(basis.at[step, pl.ds(2, 2)], *common, X_AT + 2, 2, 0, x_dev),
+            remote(basis.at[step, pl.ds(0, 2)], *common, Y_AT, 2, 1, w_dev),
+            remote(stage.at[0], *common, FAR_AT, CAP, 2, y_dev),
+            remote(stage.at[1], *common, SIB_AT, CAP, 3, sibling),
         ]
 
-    def send(basis, step, stage, ghost, sends, recvs):
-        copies = exchange(stage, ghost, sends, recvs, lax.rem(step, 2))
-        for m in (1, 3, 0, 2):
-            for e in range(CAP):
-                stage[m, e] = basis[step, send_ref[0, m, e]]
-            copies[m].start()
+    def handed(ghost, sends, recvs, parity):
+        common = (ghost, sends, recvs, parity)
+        return [
+            remote(ghost.at[parity, pl.ds(X_AT + 2, 2)], *common, Y_AT + 2, 2, 5, sibling),
+            remote(ghost.at[parity, pl.ds(Y_AT, 2)], *common, X_AT, 2, 4, sibling),
+        ]
+
+    far_slot = 3 - 2 * odd
+    sib_slot = 2 - 2 * odd
+
+    def fill(basis, step, stage, side):
+        for e in range(CAP):
+            stage[side, e] = basis[step, send_ref[e, 0, (far_slot, sib_slot)[side]]]
+
+    def send(basis, step, stage, ghost, sends, recvs, filled=False):
+        copies = direct(basis, step, stage, ghost, sends, recvs)
+        copies[1].start()
+        copies[0].start()
+        for side in range(2):
+            if not filled:
+                fill(basis, step, stage, side)
+            copies[2 + side].start()
 
     def own_table(basis, step):
         hi, lo = split_two(basis[step])
@@ -94,21 +127,38 @@
         table[0:NB, :, BLOCK:] = lo
 
     def advance(basis, step, stage, ghost, sends, recvs):
+        parity = lax.rem(step, 2)
+        copies = direct(basis, step, stage, ghost, sends, recvs)
+        relays = handed(ghost, sends, recvs, parity)
+
+        def take(at, count):
+            hi, lo = split_two(ghost[parity, at : at + count])
+            table[NB + at : NB + at + count, :, 0:BLOCK] = hi
+            table[NB + at : NB + at + count, :, BLOCK:] = lo
+
         own_table(basis, step)
-        parity = lax.rem(step, 2)
-        copies = exchange(stage, ghost, sends, recvs, parity)
-        for m in (0, 2, 1, 3):
-            copies[m].wait_recv()
-            hi, lo = split_two(ghost[parity, m])
-            at = NB + m * CAP
-            table[at : at + CAP, :, 0:BLOCK] = hi
-            table[at : at + CAP, :, BLOCK:] = lo
-        for copy in copies:
+        copies[1].wait_recv()
+        relays[1].start()
+        copies[0].wait_recv()
+        relays[0].start()
+        copies[3].wait_recv()
+        take(SIB_AT, CAP)
+        take(Y_AT, 2)
+        take(X_AT + 2, 2)
+        copies[2].wait_recv()
+        take(FAR_AT, CAP)
+        relays[1].wait_recv()
+        take(X_AT, 2)
+        relays[0].wait_recv()
+        take(Y_AT + 2, 2)
+        for copy in copies + relays:
             copy.wait_send()
         for i in range(NB):
             parts = None
             for k in range(0, SLOTS, 2):
-                pair = jnp.concatenate([table[cols_ref[i, k]], table[cols_ref[i, k + 1]]], axis=0)
+                pair = jnp.concatenate(
+                    [table[places[i * SLOTS + k]], table[places[i * SLOTS + k + 1]]], axis=0
+                )
                 term = jnp.dot(
                     mats[i, :, k * BLOCK : (k + 2) * BLOCK], pair, preferred_element_type=jnp.float32
                 )
@@ -158,10 +208,27 @@
         target[mine] = source[...]
         return jnp.sum(target[...], axis=0)
 
-    loads[0].wait()
-    send(p_basis, 0, stage_p, ghost_p, send_p, recv_p)
-    loads[1].wait()
-    send(r_basis, 0, stage_r, ghost_r, send_r, recv_r)
+    def list_copy(n, device):
+        return pltpu.make_async_remote_copy(
+            src_ref=send_vmem,
+            dst_ref=lists_v.at[n],
+            send_sem=list_send.at[n],
+            recv_sem=list_recv.at[n],
+            device_id=(device,),
+            device_id_type=MESH,
+        )
+
+    for load in lists + loads[0:2]:
+        load.wait()
+    for side in range(2):
+        fill(p_basis, 0, stage_p, side)
+        fill(r_basis, 0, stage_r, side)
+    pl.semaphore_wait(barrier, 4 + len(near_peers) + len(far_peers))
+    list_copies = [list_copy(0, x_dev), list_copy(1, w_dev)]
+    for copy in list_copies:
+        copy.start()
+    send(p_basis, 0, stage_p, ghost_p, send_p, recv_p, filled=True)
+    send(r_basis, 0, stage_r, ghost_r, send_r, recv_r, filled=True)
     loads[2].wait()
 
     rows = lax.broadcasted_iota(jnp.int32, (BLOCK, BLOCK), 0)
@@ -189,6 +256,23 @@
         ],
     )
 
+    for copy in list_copies:
+        copy.wait()
+    to_scalars = pltpu.make_async_copy(lists_v, lists_s, load_sem.at[6])
+    to_scalars.start()
+    to_scalars.wait()
+    x_slot, y_slot = 2 - 2 * odd, 1 + 2 * odd
+    for c in range(NB):
+        ghost_map[c] = c
+    for e in range(CAP):
+        ghost_map[NB + CAP * x_slot + e] = NB + X_AT + lists_s[0, e, 0, x_slot]
+        ghost_map[NB + CAP * y_slot + e] = NB + Y_AT + lists_s[1, e, 0, y_slot]
+        ghost_map[NB + CAP * (3 - 2 * odd) + e] = NB + FAR_AT + e
+        ghost_map[NB + CAP * (2 * odd) + e] = NB + SIB_AT + e
+    for i in range(NB):
+        for k in range(SLOTS):
+            places[i * SLOTS + k] = ghost_map[cols_ref[i, k]]
+
     def step_body(step, carry):
         advance(p_basis, step, stage_p, ghost_p, send_p, recv_p)
         send(p_basis, step + 1, stage_p, ghost_p, send_p, recv_p)
@@ -204,9 +288,6 @@
     lax.fori_loop(0, STEPS - 1, step_body, 0)
 
     group_start(moments, near_buf, near_send, near_recv, low, near_peers)
-    near_sum[...] = group_sum(moments, near_buf, near_send, near_recv, low, near_peers)
-    group_start(near_sum, far_buf, far_send, far_recv, high, far_peers)
-
     advance(p_basis, STEPS - 1, stage_p, ghost_p, send_p, recv_p)
     p_last = p_basis[STEPS]
     dots(
@@ -218,6 +299,8 @@
         ],
     )
     group_start(late, late_near, lnear_send, lnear_recv, low, near_peers)
+    near_sum[...] = group_sum(moments, near_buf, near_send, near_recv, low, near_peers)
+    group_start(near_sum, far_buf, far_send, far_recv, high, far_peers)
     late_sum[...] = group_sum(late, late_near, lnear_send, lnear_recv, low, near_peers)
     group_start(late_sum, late_far, lfar_send, lfar_recv, high, far_peers)
     loads[3].wait()
@@ -270,7 +353,6 @@
     coefs[1] = resid_c
     coefs[2] = direc_c
 
-    copies = []
     for i in range(NB):
         def combine(chunk, carry):
             at = pl.ds(chunk * 32, 32)
@@ -285,10 +367,15 @@
             return carry
 
         lax.fori_loop(0, BLOCK // 32, combine, 0)
-        for o, target in enumerate((point_hbm, newres_hbm, newdir_hbm)):
-            copy = pltpu.make_async_copy(outs.at[o, i], target.at[i], out_sem.at[o, i])
-            copy.start()
-            copies.append(copy)
+
+
+def deliver(outs, point_hbm, newres_hbm, newdir_hbm, sems):
+    copies = [
+        pltpu.make_async_copy(outs.at[o], target, sems.at[o])
+        for o, target in enumerate((point_hbm, newres_hbm, newdir_hbm))
+    ]
+    for copy in copies:
+        copy.start()
     for copy in copies:
         copy.wait()
 
@@ -297,14 +384,14 @@
     far_count = peers // NEAR
     blocked = (NB, BLOCK, BLOCK)
     any_space = pl.BlockSpec(memory_space=pl.ANY)
-    scalars = pl.BlockSpec(memory_space=pltpu.SMEM)
     f32 = jnp.float32
+    in_place = functools.partial(pltpu.with_memory_space_constraint, memory_space=pltpu.HBM)
     dma = pltpu.SemaphoreType.DMA
-    results = pl.pallas_call(
+    outs = pl.pallas_call(
         functools.partial(kernel, peers),
-        out_shape=[jax.ShapeDtypeStruct(blocked, f32)] * 3,
-        in_specs=[any_space, any_space, any_space, scalars, scalars, any_space],
-        out_specs=[any_space] * 3,
+        out_shape=jax.ShapeDtypeStruct((3, *blocked), f32),
+        in_specs=[any_space] * 6,
+        out_specs=pl.BlockSpec(memory_space=pltpu.VMEM),
         scratch_shapes=[
             pltpu.VMEM((STEPS + 1, *blocked), f32),
             pltpu.VMEM((STEPS, *blocked), f32),
@@ -312,11 +399,11 @@
             pltpu.VMEM((NB, SLOTS, BLOCK, BLOCK), f32),
             pltpu.VMEM((NB, 2 * BLOCK, SLOTS * BLOCK), jnp.bfloat16),
             pltpu.VMEM(blocked, f32),
-            pltpu.VMEM((NB + 4 * CAP, BLOCK, 2 * BLOCK), jnp.bfloat16),
-            pltpu.VMEM((4, CAP, BLOCK, BLOCK), f32),
-            pltpu.VMEM((4, CAP, BLOCK, BLOCK), f32),
-            pltpu.VMEM((2, 4, CAP, BLOCK, BLOCK), f32),
-            pltpu.VMEM((2, 4, CAP, BLOCK, BLOCK), f32),
+            pltpu.VMEM((NB + GHOSTS, BLOCK, 2 * BLOCK), jnp.bfloat16),
+            pltpu.VMEM((2, CAP, BLOCK, BLOCK), f32),
+            pltpu.VMEM((2, CAP, BLOCK, BLOCK), f32),
+            pltpu.VMEM((2, GHOSTS, BLOCK, BLOCK), f32),
+            pltpu.VMEM((2, GHOSTS, BLOCK, BLOCK), f32),
             pltpu.VMEM((MOMENTS, BLOCK), f32),
             pltpu.VMEM((NEAR, MOMENTS, BLOCK), f32),
             pltpu.VMEM((MOMENTS, BLOCK), f32),
@@ -328,13 +415,20 @@
             pltpu.VMEM((far_count, 8, BLOCK), f32),
             pltpu.VMEM((BASIS, 16, BLOCK), f32),
             pltpu.VMEM((3, 16, BLOCK), f32),
-            pltpu.VMEM((3, *blocked), f32),
-            dma((4,)),
-            dma((3, NB)),
-            dma((4,)),
-            dma((2, 4)),
-            dma((4,)),
-            dma((2, 4)),
+            pltpu.SMEM((NB, SLOTS), jnp.int32),
+            pltpu.SMEM((CAP, 1, 4), jnp.int32),
+            pltpu.VMEM((CAP, 1, 4), jnp.int32),
+            pltpu.VMEM((2, CAP, 1, 4), jnp.int32),
+            pltpu.SMEM((2, CAP, 1, 4), jnp.int32),
+            pltpu.SMEM((NB + 4 * CAP,), jnp.int32),
+            pltpu.SMEM((NB * SLOTS,), jnp.int32),
+            dma((8,)),
+            dma((2,)),
+            dma((2,)),
+            dma((6,)),
+            dma((2, 6)),
+            dma((6,)),
+            dma((2, 6)),
             dma((NEAR - 1,)),
             dma((NEAR,)),
             dma((far_count - 1,)),
@@ -345,17 +439,26 @@
             dma((far_count,)),
         ],
         compiler_params=pltpu.CompilerParams(
-            collective_id=0, has_side_effects=True, vmem_limit_bytes=56 * 1024 * 1024
+            collective_id=0, has_side_effects=True, vmem_limit_bytes=VMEM_GRANT
         ),
         name="cg_steps",
     )(
-        start_point.reshape(blocked),
-        residual.reshape(blocked),
-        direction.reshape(blocked),
-        send_list,
-        block_cols,
-        block_vals,
+        in_place(start_point.reshape(blocked)),
+        in_place(residual.reshape(blocked)),
+        in_place(direction.reshape(blocked)),
+        in_place(jnp.transpose(send_list, (2, 0, 1))),
+        in_place(block_cols),
+        in_place(block_vals),
     )
+    results = pl.pallas_call(
+        deliver,
+        out_shape=[jax.ShapeDtypeStruct(blocked, f32)] * 3,
+        in_specs=[pl.BlockSpec(memory_space=pltpu.VMEM)],
+        out_specs=[any_space] * 3,
+        scratch_shapes=[dma((3,))],
+        compiler_params=pltpu.CompilerParams(vmem_limit_bytes=4 * 1024 * 1024),
+        name="deliver",
+    )(outs)
     return tuple(result.reshape(NB * BLOCK, BLOCK) for result in results)
 
 

time: 104 us -> 92.4 us (0.89)
  local copies, waits for them, and re-layouts: 6.35 us -> 0 us
  Pallas kernels: 96.4 us -> 91.6 us
    unnamed x4 -> x0, local copies, waits for them, and re-layouts: 6.35 us -> none
    pallas_call x1 -> x2, Pallas kernels: 96.4 us -> 91.6 us  [the longest x1 90.7 us: shards(): pl.pallas_call(functools.partial(kernel, peers), out_shape=jax.ShapeDtype...]
where the time goes in v2:
time: 92.4 us; the launch traced here: 92.2 us
  Pallas kernels  91.6 us (99%)
    pallas_call x1, Pallas kernels, shards(): pl.pallas_call(functools.partial(kernel, peers), out_shape=jax.ShapeDtype...  90.7 us

profile of v2, /device:TPU:1, one launch (start us, length us, event | category | flops | bytes accessed | tf_op | source)
XLA Modules:
  0.0 92.2 jit_solution(13036793553728485294)
XLA Ops:
  0.6 90.7 %cg_steps.1.outs = f32[3,4,128,128]{3,2,1,0:T(8,128)S(1)} custom-call(f32[4,128,128]{2,1,0:T(8,128)} %bitcast.7, f32[4,128,128]{2,1,0:T(8,128)} %bitcast.8, f32[4,128,128]{2,1,0:T(8,128)} %bitcast.9, s32[3,1,4]{2,1,0:T(1,128)} %bitcast.10, s32[4,6]{1,0:T(4,128)} %cols_hbm.1, f32[4,6,128,128]{3,2,1,0:T(8,128)} %vals_hbm.1), custom_call_target="tpu_custom_call" | custom-call | tf_op jit(solution)/shard_map/cg_steps/pallas_call | solution.py:390
  91.3 0.9 deliver.1

commit v3 on v2

--- a/solution.py
+++ b/solution.py
@@ -35,7 +35,7 @@
     start_hbm, resid_hbm, direc_hbm, send_hbm, cols_hbm, vals_hbm,
     outs,
     p_basis, r_basis, start_v, vals_v, mats, diag, table,
-    stage_p, stage_r, ghost_p, ghost_r,
+    stage_p, stage_r, ghost_p, ghost_r, hand_p, hand_r,
     moments, near_buf, near_sum, far_buf, total, late, late_near, late_sum, late_far,
     gram, coefs, cols_ref, send_ref, send_vmem, lists_v, lists_s, ghost_map, places,
     load_sem, list_send, list_recv, send_p, recv_p, send_r, recv_r,
@@ -79,79 +79,93 @@
     for device, _ in near_peers + far_peers:
         pl.semaphore_signal(barrier, inc=1, device_id=(device,), device_id_type=MESH)
 
-    def remote(source, ghost, sends, recvs, parity, at, count, n, device):
+    def remote(source, target, sends, recvs, parity, n, device):
         return pltpu.make_async_remote_copy(
             src_ref=source,
-            dst_ref=ghost.at[parity, pl.ds(at, count)],
+            dst_ref=target,
             send_sem=sends.at[n],
             recv_sem=recvs.at[parity, n],
             device_id=(device,),
             device_id_type=MESH,
         )
 
-    def direct(basis, step, stage, ghost, sends, recvs):
-        common = (ghost, sends, recvs, lax.rem(step, 2))
-        return [
-            remote(basis.at[step, pl.ds(2, 2)], *common, X_AT + 2, 2, 0, x_dev),
-            remote(basis.at[step, pl.ds(0, 2)], *common, Y_AT, 2, 1, w_dev),
-            remote(stage.at[0], *common, FAR_AT, CAP, 2, y_dev),
-            remote(stage.at[1], *common, SIB_AT, CAP, 3, sibling),
-        ]
-
-    def handed(ghost, sends, recvs, parity):
-        common = (ghost, sends, recvs, parity)
-        return [
-            remote(ghost.at[parity, pl.ds(X_AT + 2, 2)], *common, Y_AT + 2, 2, 5, sibling),
-            remote(ghost.at[parity, pl.ds(Y_AT, 2)], *common, X_AT, 2, 4, sibling),
-        ]
+    def copies_of(chain, step):
+        basis, stage, ghost, hand, sends, recvs = chain
+        parity = lax.rem(step, 2)
+
+        def part(at, count):
+            return ghost.at[parity, pl.ds(at, count)]
+
+        def to(n, source, target, device):
+            return remote(source, target, sends, recvs, parity, n, device)
+
+        return dict(
+            upper=to(0, basis.at[step, pl.ds(2, 2)], part(X_AT + 2, 2), x_dev),
+            lower=to(1, basis.at[step, pl.ds(0, 2)], part(Y_AT, 2), w_dev),
+            onward=to(2, hand.at[parity], part(FAR_AT, CAP), x_dev),
+            beside=to(3, stage.at[1], part(SIB_AT, CAP), sibling),
+            relay_y=to(4, part(Y_AT, 2), part(X_AT, 2), sibling),
+            relay_x=to(5, part(X_AT + 2, 2), part(Y_AT + 2, 2), sibling),
+            over=to(6, stage.at[0], hand.at[parity], sibling),
+        )
 
     far_slot = 3 - 2 * odd
     sib_slot = 2 - 2 * odd
 
-    def fill(basis, step, stage, side):
+    def fill(chain, step, side):
+        basis, stage = chain[0:2]
         for e in range(CAP):
             stage[side, e] = basis[step, send_ref[e, 0, (far_slot, sib_slot)[side]]]
 
-    def send(basis, step, stage, ghost, sends, recvs, filled=False):
-        copies = direct(basis, step, stage, ghost, sends, recvs)
-        copies[1].start()
-        copies[0].start()
-        for side in range(2):
+    def send_rest(chain, step, filled=False):
+        copies = copies_of(chain, step)
+        copies["upper"].start()
+        for side, name in enumerate(("over", "beside")):
             if not filled:
-                fill(basis, step, stage, side)
-            copies[2 + side].start()
-
-    def own_table(basis, step):
-        hi, lo = split_two(basis[step])
+                fill(chain, step, side)
+            copies[name].start()
+
+    def forward(chain, step):
+        copies = copies_of(chain, step)
+        copies["over"].wait_recv()
+        copies["onward"].start()
+
+    def own_table(chain, step):
+        hi, lo = split_two(chain[0][step])
         table[0:NB, :, 0:BLOCK] = hi
         table[0:NB, :, BLOCK:] = lo
 
-    def advance(basis, step, stage, ghost, sends, recvs):
+    def advance(chain, step, more):
+        basis, ghost = chain[0], chain[2]
         parity = lax.rem(step, 2)
-        copies = direct(basis, step, stage, ghost, sends, recvs)
-        relays = handed(ghost, sends, recvs, parity)
+        copies = copies_of(chain, step)
 
         def take(at, count):
             hi, lo = split_two(ghost[parity, at : at + count])
             table[NB + at : NB + at + count, :, 0:BLOCK] = hi
             table[NB + at : NB + at + count, :, BLOCK:] = lo
 
-        own_table(basis, step)
-        copies[1].wait_recv()
-        relays[1].start()
-        copies[0].wait_recv()
-        relays[0].start()
-        copies[3].wait_recv()
+        def when_more(action):
+            if more is True:
+                action()
+            elif more is not None:
+                pl.when(more)(action)
+
+        copies["lower"].wait_recv()
+        copies["relay_y"].start()
+        copies["upper"].wait_recv()
+        copies["relay_x"].start()
+        copies["beside"].wait_recv()
         take(SIB_AT, CAP)
         take(Y_AT, 2)
         take(X_AT + 2, 2)
-        copies[2].wait_recv()
+        copies["relay_y"].wait_recv()
+        take(X_AT, 2)
+        copies["relay_x"].wait_recv()
+        take(Y_AT + 2, 2)
+        copies["onward"].wait_recv()
         take(FAR_AT, CAP)
-        relays[1].wait_recv()
-        take(X_AT, 2)
-        relays[0].wait_recv()
-        take(Y_AT + 2, 2)
-        for copy in copies + relays:
+        for copy in copies.values():
             copy.wait_send()
         for i in range(NB):
             parts = None
@@ -165,6 +179,9 @@
                 parts = term if parts is None else parts + term
             image = parts[0:BLOCK, 0:BLOCK] + (parts[0:BLOCK, BLOCK:] + parts[BLOCK:, 0:BLOCK])
             basis[step + 1, i] = image + diag[i] * basis[step, i]
+            if i == 1:
+                when_more(lambda: copies_of(chain, step + 1)["lower"].start())
+        when_more(lambda: send_rest(chain, step + 1))
 
     def dot_of(one, two):
         return jnp.sum(jnp.sum((one * two).reshape(-1, 8, BLOCK), axis=0), axis=0, keepdims=True)
@@ -220,15 +237,19 @@
 
     for load in lists + loads[0:2]:
         load.wait()
+    p_chain = (p_basis, stage_p, ghost_p, hand_p, send_p, recv_p)
+    r_chain = (r_basis, stage_r, ghost_r, hand_r, send_r, recv_r)
     for side in range(2):
-        fill(p_basis, 0, stage_p, side)
-        fill(r_basis, 0, stage_r, side)
+        fill(p_chain, 0, side)
+        fill(r_chain, 0, side)
     pl.semaphore_wait(barrier, 4 + len(near_peers) + len(far_peers))
     list_copies = [list_copy(0, x_dev), list_copy(1, w_dev)]
     for copy in list_copies:
         copy.start()
-    send(p_basis, 0, stage_p, ghost_p, send_p, recv_p, filled=True)
-    send(r_basis, 0, stage_r, ghost_r, send_r, recv_r, filled=True)
+    for chain in (p_chain, r_chain):
+        copies_of(chain, 0)["lower"].start()
+        send_rest(chain, 0, filled=True)
+        forward(chain, 0)
     loads[2].wait()
 
     rows = lax.broadcasted_iota(jnp.int32, (BLOCK, BLOCK), 0)
@@ -274,21 +295,21 @@
             places[i * SLOTS + k] = ghost_map[cols_ref[i, k]]
 
     def step_body(step, carry):
-        advance(p_basis, step, stage_p, ghost_p, send_p, recv_p)
-        send(p_basis, step + 1, stage_p, ghost_p, send_p, recv_p)
-        advance(r_basis, step, stage_r, ghost_r, send_r, recv_r)
-
-        @pl.when(step < STEPS - 2)
-        def _():
-            send(r_basis, step + 1, stage_r, ghost_r, send_r, recv_r)
-
+        own_table(p_chain, step)
+        advance(p_chain, step, True)
+        own_table(r_chain, step)
+        forward(p_chain, step + 1)
+        more = step < STEPS - 2
+        advance(r_chain, step, more)
         level(step + 1)
+        pl.when(more)(lambda: forward(r_chain, step + 1))
         return carry
 
     lax.fori_loop(0, STEPS - 1, step_body, 0)
 
     group_start(moments, near_buf, near_send, near_recv, low, near_peers)
-    advance(p_basis, STEPS - 1, stage_p, ghost_p, send_p, recv_p)
+    own_table(p_chain, STEPS - 1)
+    advance(p_chain, STEPS - 1, None)
     p_last = p_basis[STEPS]
     dots(
         late,
@@ -404,6 +425,8 @@
             pltpu.VMEM((2, CAP, BLOCK, BLOCK), f32),
             pltpu.VMEM((2, GHOSTS, BLOCK, BLOCK), f32),
             pltpu.VMEM((2, GHOSTS, BLOCK, BLOCK), f32),
+            pltpu.VMEM((2, CAP, BLOCK, BLOCK), f32),
+            pltpu.VMEM((2, CAP, BLOCK, BLOCK), f32),
             pltpu.VMEM((MOMENTS, BLOCK), f32),
             pltpu.VMEM((NEAR, MOMENTS, BLOCK), f32),
             pltpu.VMEM((MOMENTS, BLOCK), f32),
@@ -425,10 +448,10 @@
             dma((8,)),
             dma((2,)),
             dma((2,)),
-            dma((6,)),
-            dma((2, 6)),
-            dma((6,)),
-            dma((2, 6)),
+            dma((7,)),
+            dma((2, 7)),
+            dma((7,)),
+            dma((2, 7)),
             dma((NEAR - 1,)),
             dma((NEAR,)),
             dma((far_count - 1,)),

time: 92.4 us -> 82.5 us (0.89)
  Pallas kernels: 91.6 us -> 81.8 us
    pallas_call x1, Pallas kernels: 90.7 us -> 80.9 us  [shards(): pl.pallas_call(functools.partial(kernel, peers), out_shape=jax.ShapeDtype...]
where the time goes in v3:
time: 82.5 us; the launch traced here: 82.4 us
  Pallas kernels  81.8 us (99%)
    pallas_call x1, Pallas kernels, shards(): pl.pallas_call(functools.partial(kernel, peers), out_shape=jax.ShapeDtype...  80.9 us

profile of v3, /device:TPU:1, one launch (start us, length us, event | category | flops | bytes accessed | tf_op | source)
XLA Modules:
  0.0 82.4 jit_solution(13005640752960465507)
XLA Ops:
  0.6 80.9 %cg_steps.1.outs = f32[3,4,128,128]{3,2,1,0:T(8,128)S(1)} custom-call(f32[4,128,128]{2,1,0:T(8,128)} %bitcast.7, f32[4,128,128]{2,1,0:T(8,128)} %bitcast.8, f32[4,128,128]{2,1,0:T(8,128)} %bitcast.9, s32[3,1,4]{2,1,0:T(1,128)} %bitcast.10, s32[4,6]{1,0:T(4,128)} %cols_hbm.1, f32[4,6,128,128]{3,2,1,0:T(8,128)} %vals_hbm.1), custom_call_target="tpu_custom_call" | custom-call | tf_op jit(solution)/shard_map/cg_steps/pallas_call | solution.py:411
  81.5 0.9 %deliver.1 = (f32[4,128,128]{2,1,0:T(8,128)}, f32[4,128,128]{2,1,0:T(8,128)}, f32[4,128,128]{2,1,0:T(8,128)}) custom-call(f32[3,4,128,128]{3,2,1,0:T(8,128)S(1)} %cg_steps.1.outs), custom_call_target="tpu_custom_call" | custom-call | tf_op jit(solution)/shard_map/deliver/pallas_call | solution.py:476

commit v4 on v3

--- a/solution.py
+++ b/solution.py
@@ -37,7 +37,7 @@
     p_basis, r_basis, start_v, vals_v, mats, diag, table,
     stage_p, stage_r, ghost_p, ghost_r, hand_p, hand_r,
     moments, near_buf, near_sum, far_buf, total, late, late_near, late_sum, late_far,
-    gram, coefs, cols_ref, send_ref, send_vmem, lists_v, lists_s, ghost_map, places,
+    gram, coefs, moved_v, cols_ref, send_ref, send_vmem, lists_v, lists_s, ghost_map, places,
     load_sem, list_send, list_recv, send_p, recv_p, send_r, recv_r,
     near_send, near_recv, far_send, far_recv, lnear_send, lnear_recv, lfar_send, lfar_recv,
 ):
@@ -68,11 +68,17 @@
     for load in lists + loads:
         load.start()
 
-    near_peers = [(base + lax.rem(low + d, NEAR), lax.rem(low + d, NEAR)) for d in range(1, NEAR)]
-    far_peers = [
-        (lax.rem(high + d, far_count) * NEAR + low, lax.rem(high + d, far_count))
-        for d in range(1, far_count)
-    ]
+    near_peers = []
+    for hop in (2, 1, 3, 0):
+        for swap in (1, 0) if hop else (1,):
+            slot = lax.rem(low + 2 * hop, NEAR) + swap * (1 - 2 * odd)
+            near_peers.append((base + slot, slot))
+    far_peers = []
+    side_y = far_count // 4
+    ways = [(y, x) for y in range(side_y) for x in range(4) if y or x]
+    for y, x in sorted(ways, key=lambda way: -(min(way[0], side_y - way[0]) + min(way[1], 4 - way[1]))):
+        slot = lax.rem(high // 4 + y, side_y) * 4 + lax.rem(lax.rem(high, 4) + x, 4)
+        far_peers.append((slot * NEAR + low, slot))
     barrier = pltpu.get_barrier_semaphore()
     for device in (x_dev, y_dev, w_dev, sibling):
         pl.semaphore_signal(barrier, inc=1, device_id=(device,), device_id_type=MESH)
@@ -326,14 +332,12 @@
     group_start(late_sum, late_far, lfar_send, lfar_recv, high, far_peers)
     loads[3].wait()
     total[...] = group_sum(near_sum, far_buf, far_send, far_recv, high, far_peers)
-    last = group_sum(late_sum, late_far, lfar_send, lfar_recv, high, far_peers)
-    total[PP + 11 : PP + 13, :] = last[0:2]
-    pr_last = last[2:3]
+    unknown = jnp.zeros((1, BLOCK), jnp.float32)
 
     def pr_rows(first, count):
         wanted = min(first + count, 11) - first
         part = total[PR + first : PR + first + wanted, :]
-        return part if wanted == count else jnp.concatenate([part, pr_last], axis=0)
+        return part if wanted == count else jnp.concatenate([part, unknown], axis=0)
 
     for b in range(STEPS + 1):
         gram[b, 0 : STEPS + 1, :] = total[PP + b : PP + b + STEPS + 1, :]
@@ -342,8 +346,8 @@
         gram[STEPS + 1 + b, 0 : STEPS + 1, :] = pr_rows(b, STEPS + 1)
         gram[STEPS + 1 + b, STEPS + 1 : BASIS, :] = total[RR + b : RR + b + STEPS, :]
 
-    places = lax.broadcasted_iota(jnp.int32, (16, BLOCK), 0)
-    active = (places < STEPS) | ((places > STEPS) & (places < BASIS - 1))
+    indices = lax.broadcasted_iota(jnp.int32, (16, BLOCK), 0)
+    active = (indices < STEPS) | ((indices > STEPS) & (indices < BASIS - 1))
 
     def times_gram(vector):
         sums = [gram[b] * vector[b : b + 1, :] for b in range(BASIS)]
@@ -356,38 +360,70 @@
     def inner(one, two):
         return jnp.sum(one * two, axis=0, keepdims=True)
 
+    def moved_by(vector):
+        held = jnp.where(active, vector, 0.0)
+        shifted = jnp.concatenate([jnp.zeros((1, BLOCK), jnp.float32), held[0:15]], axis=0)
+        return center_value * held + half_range * shifted
+
     point_c = jnp.zeros((16, BLOCK), jnp.float32)
-    resid_c = jnp.where(places == STEPS + 1, 1.0, 0.0).astype(jnp.float32)
-    direc_c = jnp.where(places == 0, 1.0, 0.0).astype(jnp.float32)
+    resid_c = jnp.where(indices == STEPS + 1, 1.0, 0.0).astype(jnp.float32)
+    direc_c = jnp.where(indices == 0, 1.0, 0.0).astype(jnp.float32)
     current = inner(resid_c, times_gram(resid_c))
-    for _ in range(STEPS):
-        held = jnp.where(active, direc_c, 0.0)
-        shifted = jnp.concatenate([jnp.zeros((1, BLOCK), jnp.float32), held[0:15]], axis=0)
-        moved = center_value * held + half_range * shifted
+    for _ in range(STEPS - 1):
+        moved = moved_by(direc_c)
         alpha = current / inner(direc_c, times_gram(moved))
         point_c = point_c + alpha * direc_c
         resid_c = resid_c - alpha * moved
         following = inner(resid_c, times_gram(resid_c))
         direc_c = resid_c + (following / current) * direc_c
         current = following
-    coefs[0] = point_c
-    coefs[1] = resid_c
-    coefs[2] = direc_c
+    moved = moved_by(direc_c)
+    image = times_gram(moved)
+    curvature = inner(direc_c, image)
+    mixed = inner(resid_c, image)
+    square = inner(moved, image)
+    top = moved[STEPS : STEPS + 1]
+    below = moved[STEPS - 1 : STEPS]
+    last_r = moved[BASIS - 1 : BASIS]
+    direc_top = direc_c[STEPS - 1 : STEPS]
+    resid_top = resid_c[STEPS - 1 : STEPS]
+    for o, vector in enumerate((point_c, resid_c, direc_c, moved)):
+        coefs[o] = vector
 
     for i in range(NB):
         def combine(chunk, carry):
             at = pl.ds(chunk * 32, 32)
-            sums = [start_v[i, at, :], None, None]
+            sums = [start_v[i, at, :], None, None, None]
             for a in range(BASIS):
                 piece = p_basis[a, i, at, :] if a <= STEPS else r_basis[a - STEPS - 1, i, at, :]
-                for o in range(3):
+                for o in range(4):
                     term = coefs[o, a : a + 1, :] * piece
                     sums[o] = term if sums[o] is None else sums[o] + term
             for o in range(3):
                 outs[o, i, at, :] = sums[o]
+            moved_v[i, at, :] = sums[3]
             return carry
 
         lax.fori_loop(0, BLOCK // 32, combine, 0)
+
+    last = group_sum(late_sum, late_far, lfar_send, lfar_recv, high, far_peers)
+    pp_low, pp_high, pr_high = last[0:1], last[1:2], last[2:3]
+    curvature = curvature + direc_top * (top * pp_low)
+    mixed = mixed + resid_top * (top * pp_low)
+    square = square + top * (2.0 * (below * pp_low + last_r * pr_high) + top * pp_high)
+    alpha = current / curvature
+    following = current - alpha * (2.0 * mixed - alpha * square)
+    beta = following / current
+
+    def finish(i, carry):
+        old = outs[2, i]
+        outs[0, i] = outs[0, i] + alpha * old
+        fresh = outs[1, i] - alpha * moved_v[i]
+        outs[1, i] = fresh
+        outs[2, i] = fresh + beta * old
+        return carry
+
+    lax.fori_loop(0, NB, finish, 0)
 
 
 def deliver(outs, point_hbm, newres_hbm, newdir_hbm, sems):
@@ -437,7 +473,8 @@
             pltpu.VMEM((8, BLOCK), f32),
             pltpu.VMEM((far_count, 8, BLOCK), f32),
             pltpu.VMEM((BASIS, 16, BLOCK), f32),
-            pltpu.VMEM((3, 16, BLOCK), f32),
+            pltpu.VMEM((4, 16, BLOCK), f32),
+            pltpu.VMEM(blocked, f32),
             pltpu.SMEM((NB, SLOTS), jnp.int32),
             pltpu.SMEM((CAP, 1, 4), jnp.int32),
             pltpu.VMEM((CAP, 1, 4), jnp.int32),

time: 82.5 us -> 81.5 us (0.988)
  Pallas kernels: 81.8 us -> 80.7 us
    pallas_call x1, Pallas kernels: 80.9 us -> 79.8 us  [shards(): pl.pallas_call(functools.partial(kernel, peers), out_shape=jax.ShapeDtype...]
where the time goes in v4:
time: 81.5 us; the launch traced here: 81.4 us
  Pallas kernels  80.7 us (99%)
    pallas_call x1, Pallas kernels, shards(): pl.pallas_call(functools.partial(kernel, peers), out_shape=jax.ShapeDtype...  79.8 us

profile of v4, /device:TPU:1, one launch (start us, length us, event | category | flops | bytes accessed | tf_op | source)
XLA Modules:
  0.0 81.4 jit_solution(7252962077380304897)
XLA Ops:
  0.6 79.8 %cg_steps.1.outs = f32[3,4,128,128]{3,2,1,0:T(8,128)S(1)} custom-call(f32[4,128,128]{2,1,0:T(8,128)} %bitcast.7, f32[4,128,128]{2,1,0:T(8,128)} %bitcast.8, f32[4,128,128]{2,1,0:T(8,128)} %bitcast.9, s32[3,1,4]{2,1,0:T(1,128)} %bitcast.10, s32[4,6]{1,0:T(4,128)} %cols_hbm.1, f32[4,6,128,128]{3,2,1,0:T(8,128)} %vals_hbm.1), custom_call_target="tpu_custom_call" | custom-call | tf_op jit(solution)/shard_map/cg_steps/pallas_call | solution.py:447
  80.5 0.9 %deliver.1 = (f32[4,128,128]{2,1,0:T(8,128)}, f32[4,128,128]{2,1,0:T(8,128)}, f32[4,128,128]{2,1,0:T(8,128)}) custom-call(f32[3,4,128,128]{3,2,1,0:T(8,128)S(1)} %cg_steps.1.outs), custom_call_target="tpu_custom_call" | custom-call | tf_op jit(solution)/shard_map/deliver/pallas_call | solution.py:513

commit v5 on v4

--- a/solution.py
+++ b/solution.py
@@ -34,7 +34,7 @@
     peers,
     start_hbm, resid_hbm, direc_hbm, send_hbm, cols_hbm, vals_hbm,
     outs,
-    p_basis, r_basis, start_v, vals_v, mats, diag, table,
+    p_basis, r_basis, start_v, vals_v, mats, far_mats, diag, table,
     stage_p, stage_r, ghost_p, ghost_r, hand_p, hand_r,
     moments, near_buf, near_sum, far_buf, total, late, late_near, late_sum, late_far,
     gram, coefs, moved_v, cols_ref, send_ref, send_vmem, lists_v, lists_s, ghost_map, places,
@@ -141,6 +141,9 @@
         table[0:NB, :, 0:BLOCK] = hi
         table[0:NB, :, BLOCK:] = lo
 
+    def joined(parts):
+        return parts[0:BLOCK, 0:BLOCK] + (parts[0:BLOCK, BLOCK:] + parts[BLOCK:, 0:BLOCK])
+
     def advance(chain, step, more):
         basis, ghost = chain[0], chain[2]
         parity = lax.rem(step, 2)
@@ -169,23 +172,25 @@
         take(X_AT, 2)
         copies["relay_x"].wait_recv()
         take(Y_AT + 2, 2)
+        for i in range(NB):
+            picked = [table[places[i * SLOTS + k]] for k in range(SLOTS)]
+            parts = jnp.dot(
+                mats[i], jnp.concatenate(picked, axis=0), preferred_element_type=jnp.float32
+            )
+            basis[step + 1, i] = joined(parts) + diag[i] * basis[step, i]
         copies["onward"].wait_recv()
         take(FAR_AT, CAP)
         for copy in copies.values():
             copy.wait_send()
-        for i in range(NB):
-            parts = None
-            for k in range(0, SLOTS, 2):
-                pair = jnp.concatenate(
-                    [table[places[i * SLOTS + k]], table[places[i * SLOTS + k + 1]]], axis=0
-                )
-                term = jnp.dot(
-                    mats[i, :, k * BLOCK : (k + 2) * BLOCK], pair, preferred_element_type=jnp.float32
-                )
-                parts = term if parts is None else parts + term
-            image = parts[0:BLOCK, 0:BLOCK] + (parts[0:BLOCK, BLOCK:] + parts[BLOCK:, 0:BLOCK])
-            basis[step + 1, i] = image + diag[i] * basis[step, i]
-            if i == 1:
+        far = table[NB + FAR_AT : NB + FAR_AT + CAP].reshape(CAP * BLOCK, 2 * BLOCK)
+        for half in range(2):
+            rows_of = slice(half * 4 * BLOCK, (half + 1) * 4 * BLOCK)
+            parts = jnp.dot(far_mats[rows_of], far, preferred_element_type=jnp.float32)
+            for j in range(2):
+                i = 2 * half + j
+                part = parts[2 * j * BLOCK : 2 * (j + 1) * BLOCK]
+                basis[step + 1, i] = basis[step + 1, i] + joined(part)
+            if half == 0:
                 when_more(lambda: copies_of(chain, step + 1)["lower"].start())
         when_more(lambda: send_rest(chain, step + 1))
 
@@ -271,6 +276,17 @@
             hi, lo = split_two(values * (1.0 / half_range))
             mats[i, 0:BLOCK, k * BLOCK : (k + 1) * BLOCK] = hi
             mats[i, BLOCK:, k * BLOCK : (k + 1) * BLOCK] = lo
+    table[NB + GHOSTS] = jnp.zeros((BLOCK, 2 * BLOCK), jnp.bfloat16)
+    for i in range(NB):
+        for e in range(CAP):
+            wanted = NB + CAP * far_slot + e
+            values = jnp.zeros((BLOCK, BLOCK), jnp.float32)
+            for k in range(1, SLOTS):
+                values = values + jnp.where(cols_ref[i, k] == wanted, vals_v[i, k], 0.0)
+            hi, lo = split_two(values * (1.0 / half_range))
+            at = 2 * i * BLOCK
+            far_mats[at : at + BLOCK, e * BLOCK : (e + 1) * BLOCK] = hi
+            far_mats[at + BLOCK : at + 2 * BLOCK, e * BLOCK : (e + 1) * BLOCK] = lo
     moments[...] = jnp.zeros_like(moments)
     late[...] = jnp.zeros_like(late)
     gram[...] = jnp.zeros_like(gram)
@@ -294,7 +310,7 @@
     for e in range(CAP):
         ghost_map[NB + CAP * x_slot + e] = NB + X_AT + lists_s[0, e, 0, x_slot]
         ghost_map[NB + CAP * y_slot + e] = NB + Y_AT + lists_s[1, e, 0, y_slot]
-        ghost_map[NB + CAP * (3 - 2 * odd) + e] = NB + FAR_AT + e
+        ghost_map[NB + CAP * far_slot + e] = NB + GHOSTS
         ghost_map[NB + CAP * (2 * odd) + e] = NB + SIB_AT + e
     for i in range(NB):
         for k in range(SLOTS):
@@ -455,8 +471,9 @@
             pltpu.VMEM(blocked, f32),
             pltpu.VMEM((NB, SLOTS, BLOCK, BLOCK), f32),
             pltpu.VMEM((NB, 2 * BLOCK, SLOTS * BLOCK), jnp.bfloat16),
+            pltpu.VMEM((NB * 2 * BLOCK, CAP * BLOCK), jnp.bfloat16),
             pltpu.VMEM(blocked, f32),
-            pltpu.VMEM((NB + GHOSTS, BLOCK, 2 * BLOCK), jnp.bfloat16),
+            pltpu.VMEM((NB + GHOSTS + 1, BLOCK, 2 * BLOCK), jnp.bfloat16),
             pltpu.VMEM((2, CAP, BLOCK, BLOCK), f32),
             pltpu.VMEM((2, CAP, BLOCK, BLOCK), f32),
             pltpu.VMEM((2, GHOSTS, BLOCK, BLOCK), f32),

time: 81.5 us -> 81.6 us (level)
  no operation moved by 1% of the time
where the time goes in v5:
time: 81.6 us; the launch traced here: 81.4 us
  Pallas kernels  80.8 us (99%)
    pallas_call x1, Pallas kernels, shards(): pl.pallas_call(functools.partial(kernel, peers), out_shape=jax.ShapeDtype...  79.9 us

profile of v5, /device:TPU:1, one launch (start us, length us, event | category | flops | bytes accessed | tf_op | source)
XLA Modules:
  0.0 81.4 jit_solution(4498088721099694150)
XLA Ops:
  0.6 79.9 %cg_steps.1.outs = f32[3,4,128,128]{3,2,1,0:T(8,128)S(1)} custom-call(f32[4,128,128]{2,1,0:T(8,128)} %bitcast.7, f32[4,128,128]{2,1,0:T(8,128)} %bitcast.8, f32[4,128,128]{2,1,0:T(8,128)} %bitcast.9, s32[3,1,4]{2,1,0:T(1,128)} %bitcast.10, s32[4,6]{1,0:T(4,128)} %cols_hbm.1, f32[4,6,128,128]{3,2,1,0:T(8,128)} %vals_hbm.1), custom_call_target="tpu_custom_call" | custom-call | tf_op jit(solution)/shard_map/cg_steps/pallas_call | solution.py:463
  80.5 0.9 %deliver.1 = (f32[4,128,128]{2,1,0:T(8,128)}, f32[4,128,128]{2,1,0:T(8,128)}, f32[4,128,128]{2,1,0:T(8,128)}) custom-call(f32[3,4,128,128]{3,2,1,0:T(8,128)S(1)} %cg_steps.1.outs), custom_call_target="tpu_custom_call" | custom-call | tf_op jit(solution)/shard_map/deliver/pallas_call | solution.py:530

commit v6 on v4

--- a/solution.py
+++ b/solution.py
@@ -106,9 +106,12 @@
             return remote(source, target, sends, recvs, parity, n, device)
 
         return dict(
-            upper=to(0, basis.at[step, pl.ds(2, 2)], part(X_AT + 2, 2), x_dev),
-            lower=to(1, basis.at[step, pl.ds(0, 2)], part(Y_AT, 2), w_dev),
-            onward=to(2, hand.at[parity], part(FAR_AT, CAP), x_dev),
+            lower=to(1, basis.at[step, pl.ds(0, 1)], part(Y_AT, 1), w_dev),
+            lower_b=to(7, basis.at[step, pl.ds(1, 1)], part(Y_AT + 1, 1), w_dev),
+            upper=to(0, basis.at[step, pl.ds(2, 1)], part(X_AT + 2, 1), x_dev),
+            upper_b=to(8, basis.at[step, pl.ds(3, 1)], part(X_AT + 3, 1), x_dev),
+            onward=to(2, hand.at[parity, pl.ds(0, 2)], part(FAR_AT, 2), x_dev),
+            onward_b=to(9, hand.at[parity, pl.ds(2, 1)], part(FAR_AT + 2, 1), x_dev),
             beside=to(3, stage.at[1], part(SIB_AT, CAP), sibling),
             relay_y=to(4, part(Y_AT, 2), part(X_AT, 2), sibling),
             relay_x=to(5, part(X_AT + 2, 2), part(Y_AT + 2, 2), sibling),
@@ -125,7 +128,7 @@
 
     def send_rest(chain, step, filled=False):
         copies = copies_of(chain, step)
-        copies["upper"].start()
+        copies["upper_b"].start()
         for side, name in enumerate(("over", "beside")):
             if not filled:
                 fill(chain, step, side)
@@ -135,6 +138,7 @@
         copies = copies_of(chain, step)
         copies["over"].wait_recv()
         copies["onward"].start()
+        copies["onward_b"].start()
 
     def own_table(chain, step):
         hi, lo = split_two(chain[0][step])
@@ -158,8 +162,10 @@
                 pl.when(more)(action)
 
         copies["lower"].wait_recv()
+        copies["lower_b"].wait_recv()
         copies["relay_y"].start()
         copies["upper"].wait_recv()
+        copies["upper_b"].wait_recv()
         copies["relay_x"].start()
         copies["beside"].wait_recv()
         take(SIB_AT, CAP)
@@ -170,9 +176,12 @@
         copies["relay_x"].wait_recv()
         take(Y_AT + 2, 2)
         copies["onward"].wait_recv()
-        take(FAR_AT, CAP)
-        for copy in copies.values():
-            copy.wait_send()
+        take(FAR_AT, 2)
+        copies["onward_b"].wait_recv()
+        take(FAR_AT + 2, 1)
+        names = list(copies)
+        for name in names[0:4]:
+            copies[name].wait_send()
         for i in range(NB):
             parts = None
             for k in range(0, SLOTS, 2):
@@ -185,8 +194,11 @@
                 parts = term if parts is None else parts + term
             image = parts[0:BLOCK, 0:BLOCK] + (parts[0:BLOCK, BLOCK:] + parts[BLOCK:, 0:BLOCK])
             basis[step + 1, i] = image + diag[i] * basis[step, i]
-            if i == 1:
-                when_more(lambda: copies_of(chain, step + 1)["lower"].start())
+            if i < 3:
+                name = ("lower", "lower_b", "upper")[i]
+                when_more(lambda: copies_of(chain, step + 1)[name].start())
+        for name in names[4:]:
+            copies[name].wait_send()
         when_more(lambda: send_rest(chain, step + 1))
 
     def dot_of(one, two):
@@ -253,7 +265,8 @@
     for copy in list_copies:
         copy.start()
     for chain in (p_chain, r_chain):
-        copies_of(chain, 0)["lower"].start()
+        for name in ("lower", "lower_b", "upper"):
+            copies_of(chain, 0)[name].start()
         send_rest(chain, 0, filled=True)
         forward(chain, 0)
     loads[2].wait()
@@ -485,10 +498,10 @@
             dma((8,)),
             dma((2,)),
             dma((2,)),
-            dma((7,)),
-            dma((2, 7)),
-            dma((7,)),
-            dma((2, 7)),
+            dma((10,)),
+            dma((2, 10)),
+            dma((10,)),
+            dma((2, 10)),
             dma((NEAR - 1,)),
             dma((NEAR,)),
             dma((far_count - 1,)),

time: 81.5 us -> 81.4 us (level)
  no operation moved by 1% of the time
where the time goes in v6:
time: 81.4 us; the launch traced here: 81.3 us
  Pallas kernels  80.6 us (99%)
    pallas_call x1, Pallas kernels, shards(): pl.pallas_call(functools.partial(kernel, peers), out_shape=jax.ShapeDtype...  79.7 us

profile of v6, /device:TPU:1, one launch (start us, length us, event | category | flops | bytes accessed | tf_op | source)
XLA Modules:
  0.0 81.3 jit_solution(12791410033385643520)
XLA Ops:
  0.6 79.7 %cg_steps.1.outs = f32[3,4,128,128]{3,2,1,0:T(8,128)S(1)} custom-call(f32[4,128,128]{2,1,0:T(8,128)} %bitcast.7, f32[4,128,128]{2,1,0:T(8,128)} %bitcast.8, f32[4,128,128]{2,1,0:T(8,128)} %bitcast.9, s32[3,1,4]{2,1,0:T(1,128)} %bitcast.10, s32[4,6]{1,0:T(4,128)} %cols_hbm.1, f32[4,6,128,128]{3,2,1,0:T(8,128)} %vals_hbm.1), custom_call_target="tpu_custom_call" | custom-call | tf_op jit(solution)/shard_map/cg_steps/pallas_call | solution.py:460
  80.4 0.9 %deliver.1 = (f32[4,128,128]{2,1,0:T(8,128)}, f32[4,128,128]{2,1,0:T(8,128)}, f32[4,128,128]{2,1,0:T(8,128)}) custom-call(f32[3,4,128,128]{3,2,1,0:T(8,128)S(1)} %cg_steps.1.outs), custom_call_target="tpu_custom_call" | custom-call | tf_op jit(solution)/shard_map/deliver/pallas_call | solution.py:526
